TPU v7x, 256 devices: a whole 4x4x8 slice. The times are simulated.
256 devices in a mesh: batch: 16 (over y, x), field: 2 (over core), dim: 8 (over z).
Axes of the slice: x: 4, y: 4, z: 8, core: 2. Of those that a mesh axis runs over, the one named last changes fastest.
Arguments:
- features: bfloat16 [26, 128, 16384], P('field', 'dim', 'batch'), may hold values from -6 to 6
- cross_weight: bfloat16 [2, 26, 128, 26, 128], P(None, 'field', 'dim'), may hold values from -0.109375 to 0.109375
- cross_bias: float32 [2, 26, 128], P(None, 'field', 'dim'), may hold values from -3 to 3
- tower_weight: bfloat16 [1024, 26, 128], P(('field', 'dim')), may hold values from -0.109375 to 0.109375
- tower_bias: float32 [1024], P(('field', 'dim')), may hold values from -3 to 3
- query_weight: bfloat16 [1024, 128], P(('field', 'dim')), may hold values from -0.1875 to 0.1875
- user_vec: bfloat16 [16384, 128], P('batch'), may hold values from -6 to 6
- candidates: bfloat16 [4096, 128], P('batch'), may hold values from -6 to 6
- positive: int32 [16384], P('batch'), may hold values from 0 to 4095
Outputs:
- crossed: bfloat16 [26, 128, 16384], P('field', 'dim', 'batch')
- losses: float32 [16384], P('batch')
All inputs are finite; a program needn't handle non-finite values.
Results may differ from a plain program's by a relative error of at most 0.0049.
Values may be sent and summed in bfloat16 or wider, within the bound.
A program may use at most 64 MiB of HBM per device.

v0:
```python
import math

import jax
import jax.numpy as jnp
from jax import lax
from jax.sharding import Mesh
from jax.sharding import PartitionSpec as P

CROSS = 2
BATCH = ("batch_0", "batch_1")


def whole_of(x, axes, dim):
    if not axes:
        return x
    nearer = lax.all_gather(x, axes[-1], axis=dim, tiled=True)
    return whole_of(nearer, axes[:-1], dim)


def cut_along(x, dim, length):
    shape = x.shape
    pieces = x.reshape(*shape[:dim], length, shape[dim] // length, *shape[dim + 1 :])
    return jnp.moveaxis(pieces, dim, 0)


def summed_on_arrival(x, axis, dim):
    length = lax.axis_size(axis)
    pieces = lax.all_to_all(cut_along(x, dim, length), axis, 0, 0, tiled=True)
    return jnp.sum(pieces.astype(jnp.float32), axis=0)


def laid_out(pieces, dim):
    shape = list(pieces.shape[1:])
    shape[dim] *= pieces.shape[0]
    return jnp.moveaxis(pieces, 0, dim).reshape(shape)


def sent_to_all(x, axis):
    copies = jnp.broadcast_to(x, (lax.axis_size(axis), *x.shape))
    return lax.all_to_all(copies, axis, split_axis=0, concat_axis=0, tiled=True)


def gather_directly(x, axis, dim):
    return laid_out(sent_to_all(x, axis), dim)


def by_device(weights, field_count, dim_count):
    out_count, fields_all, entries_all = weights.shape
    shaped = weights.reshape(
        out_count, field_count, fields_all // field_count, dim_count, entries_all // dim_count
    )
    shaped = shaped.transpose(1, 3, 0, 2, 4)
    return shaped.reshape(
        field_count * dim_count, out_count, fields_all // field_count * (entries_all // dim_count)
    )


def row_adder(blocks, shards):
    return jnp.einsum("kib,koi->ob", shards, blocks, preferred_element_type=jnp.float32)


def cross_flat(current, blocks):
    field_local, entry_local, row_count = current.shape
    flattened = current.reshape(1, field_local * entry_local, row_count)
    return row_adder(blocks, lax.all_gather(flattened, ("field", "dim"), axis=0, tiled=True))


def next_layer(anchor, current, product, bias_vec):
    field_local, entry_local, row_count = current.shape
    gated = (product + bias_vec.reshape(field_local * entry_local, 1)).reshape(
        field_local, entry_local, row_count
    )
    return (anchor * gated + current.astype(jnp.float32)).astype(jnp.bfloat16)


def candidate_loss(query_vec, targets, candidates):
    score_scale = 1.0 / math.sqrt(query_vec.shape[1])
    row_count = query_vec.shape[0]
    running_max = jnp.full((row_count,), -1e30, jnp.float32)
    logits = (
        jnp.einsum(
            "be,ce->bc",
            query_vec,
            whole_of(candidates, BATCH, 0),
            preferred_element_type=jnp.float32,
        )
        * score_scale
    )
    labels = lax.broadcasted_iota(jnp.int32, logits.shape, 1)
    picked = jnp.sum(jnp.where(labels == targets[:, None], logits, 0.0), axis=1)
    new_max = jnp.maximum(running_max, jnp.max(logits, axis=1))
    running_sum = jnp.sum(jnp.exp(logits - new_max[:, None]), axis=1)
    best_score, exp_total, picked = (new_max, running_sum, picked)
    return best_score + jnp.log(exp_total) - picked


def body(
    features,
    cross_weight,
    cross_bias,
    tower_weight,
    tower_bias,
    query_weight,
    user_vec,
    candidates,
    positive,
):
    field_count = lax.axis_size("field")
    dim_count = lax.axis_size("dim")
    field_local, entry_local, row_count = features.shape
    column_count = field_local * entry_local
    anchor = features.astype(jnp.float32)
    current = features
    stacked = cross_weight.reshape(
        CROSS, column_count, cross_weight.shape[3], cross_weight.shape[4]
    )
    for level_idx in range(CROSS):
        blocks = by_device(stacked[level_idx], field_count, dim_count)
        product = cross_flat(current, blocks)
        current = next_layer(anchor, current, product, cross_bias[level_idx])
    tower_blocks = by_device(tower_weight, field_count, dim_count)
    flattened = current.reshape(1, column_count, row_count)
    tower_pre = row_adder(
        tower_blocks, lax.all_gather(flattened, ("field", "dim"), axis=0, tiled=True)
    )
    hidden = jax.nn.relu(tower_pre + tower_bias[:, None]).astype(jnp.bfloat16)
    partial_value = lax.dot_general(
        hidden, query_weight, (((0,), (0,)), ((), ())), preferred_element_type=jnp.float32
    )
    share_rows = row_count // (field_count * dim_count)
    member = lax.axis_index(("field", "dim"))
    query_part = summed_on_arrival(partial_value.astype(jnp.bfloat16), ("field", "dim"), 0)
    user_rows = lax.dynamic_slice_in_dim(user_vec, member * share_rows, share_rows, 0)
    targets = lax.dynamic_slice_in_dim(positive, member * share_rows, share_rows, 0)
    query_vec = (query_part + user_rows.astype(jnp.float32)).astype(jnp.bfloat16)
    part_loss = candidate_loss(query_vec, targets, candidates)
    losses = gather_directly(part_loss, ("field", "dim"), 0)
    return (current, losses)


def solution(mesh):
    torus = Mesh(
        mesh.devices.reshape(4, 4, mesh.shape["field"], mesh.shape["dim"]),
        ("batch_0", "batch_1", "field", "dim"),
    )
    in_specs = (
        P("field", "dim", BATCH),
        P(None, "field", "dim", None, None),
        P(None, "field", "dim"),
        P(("field", "dim"), None, None),
        P(("field", "dim")),
        P(("field", "dim"), None),
        P(BATCH, None),
        P(BATCH, None),
        P(BATCH),
    )
    out_specs = (P("field", "dim", BATCH), P(BATCH))
    return jax.shard_map(body, mesh=torus, in_specs=in_specs, out_specs=out_specs, check_vma=False)
```

profile of v0, /device:TPU:7, one launch (start us, length us, event | category | flops | bytes accessed | tf_op | source)
XLA Modules:
  0.0 218.9 jit_solution(14988092904554589448)
XLA Ops:
  7.2 0.7 all-gather.5.cloned.1.call-update
  8.0 2.2 %fusion.13 = (bf16[1,13,16,26,128]{4,2,3,1,0:T(8,128)(2,1)S(1)}, bf16[1,13,16,26,128]{4,2,3,1,0:T(8,128)(2,1)S(1)}) fusion(bf16[2,13,16,26,128]{4,2,3,1,0:T(8,128)(2,1)} %param.10), kind=kLoop, calls=%fused_computation.29 | loop fusion | bytes 5537792 | tf_op jit(solution)/shard_map/slice | solution.py:118
  10.4 8.7 %reshape_squeeze.8 = bf16[208,2,13,8,16]{4,3,0,2,1:T(8,128)(2,1)} reshape(bf16[1,13,16,26,128]{4,2,1,3,0:T(8,128)(2,1)S(1)} %copy.19) | data formatting | bytes 2768896 | tf_op jit(solution)/shard_map/reshape;squeeze | solution.py:49
  19.1 10.9 %copy.20 = bf16[2,8,208,13,16]{2,4,3,1,0:T(8,128)(2,1)S(1)} copy(bf16[2,8,208,13,16]{4,1,2,3,0:T(8,128)(2,1)} %bitcast.50) | data formatting | bytes 2768896 | tf_op jit(solution)/shard_map/transpose | solution.py:52
  30.2 31.4 %all-gather.5.cloned.1.call-done = bf16[16,208,1024]{2,1,0:T(8,128)(2,1)} async-done(((bf16[1,208,1024]{2,1,0:T(8,128)(2,1)}), bf16[16,208,1024]{2,1,0:T(8,128)(2,1)}) %all-gather.5.cloned.1.call-update) | async-done | bytes 6815760 | tf_op jit(solution)/shard_map/all_gather | solution.py:65
  61.6 4.6 %fusion = f32[208,1024]{1,0:T(8,128)S(1)} fusion(bf16[16,208,208]{1,2,0:T(8,128)(2,1)S(1)} %bitcast.52, bf16[16,208,1024]{2,1,0:T(8,128)(2,1)} %all-gather.5.cloned.1.call-done, f32[208]{0:T(256)S(1)} %add.51), kind=kOutput, calls=%fused_computation.4 | convolution fusion | flops 1417887744 | bytes 9052992 | tf_op jit(solution)/shard_map/kib,koi->ob/dot_general | solution.py:59
  66.2 0.9 fusion.7
  67.4 8.7 %reshape_squeeze.9 = bf16[208,2,13,8,16]{4,3,0,2,1:T(8,128)(2,1)} reshape(bf16[1,13,16,26,128]{4,2,1,3,0:T(8,128)(2,1)S(1)} %copy.22) | data formatting | bytes 2768896 | tf_op jit(solution)/shard_map/reshape;squeeze | solution.py:49
  76.1 11.1 %copy.23 = bf16[2,8,208,13,16]{2,4,3,1,0:T(8,128)(2,1)S(1)} copy(bf16[2,8,208,13,16]{4,1,2,3,0:T(8,128)(2,1)} %bitcast.51) | data formatting | bytes 2768896 | tf_op jit(solution)/shard_map/transpose | solution.py:52
  87.3 27.0 %all-gather.7.cloned.1.call-done = bf16[16,208,1024]{2,1,0:T(8,128)(2,1)} async-done(((bf16[1,208,1024]{2,1,0:T(8,128)(2,1)}), bf16[16,208,1024]{2,1,0:T(8,128)(2,1)}) %all-gather.7.cloned.1.call-update) | async-done | bytes 6815760 | tf_op jit(solution)/shard_map/all_gather | solution.py:65
  114.3 4.6 %fusion.1 = f32[1024,208]{0,1:T(8,128)S(1)} fusion(bf16[16,208,1024]{2,1,0:T(8,128)(2,1)} %all-gather.7.cloned.1.call-done, bf16[16,208,208]{1,2,0:T(8,128)(2,1)S(1)} %bitcast.58, f32[208]{0:T(256)S(1)} %add.55), kind=kOutput, calls=%fused_computation.5 | convolution fusion | flops 1417887744 | bytes 9052992 | tf_op jit(solution)/shard_map/kib,koi->ob/dot_general | solution.py:59
  119.0 1.0 fusion.6
  120.0 10.1 %all_gather.18 = bf16[1024,128]{1,0:T(8,128)(2,1)} all-gather(bf16[256,128]{1,0:T(8,128)(2,1)S(1)} %copy-done.4), channel_id=1, replica_groups=mesh['batch_0'=4,'batch_1'=4,'field'=2,'dim'=8] {'batch_1'}, dimensions={0}, use_global_device_ids=true | all-gather | bytes 327680 | tf_op jit(solution)/shard_map/all_gather | solution.py:16
  130.7 36.4 %all-gather.9.cloned.1.call-done = bf16[16,208,1024]{2,1,0:T(8,128)(2,1)} async-done(((bf16[1,208,1024]{2,1,0:T(8,128)(2,1)}), bf16[16,208,1024]{2,1,0:T(8,128)(2,1)}) %all-gather.9.cloned.1.call-update) | async-done | bytes 6815760 | tf_op jit(solution)/shard_map/all_gather | solution.py:124
  167.1 5.3 %convolution_convert_fusion = bf16[1024,128]{1,0:T(8,128)(2,1)} fusion(bf16[64,128]{1,0:T(8,128)(2,1)S(1)} %copy-done, bf16[16,208,1024]{2,1,0:T(8,128)(2,1)} %all-gather.9.cloned.1.call-done, bf16[16,64,208]{1,2,0:T(8,128)(2,1)S(1)} %bitcast.56, f32[64]{0:T(128)S(1)} %copy-done.6), kind=kOutput, calls=%fused_computation.6 | convolution fusion | flops 453312512 | bytes 7520512 | tf_op jit(solution)/shard_map/dot_general | solution.py:127
  172.4 4.6 %all-to-all-start = ((bf16[16,64,128]{2,1,0:T(8,128)(2,1)}), bf16[16,64,128]{2,1,0:T(8,128)(2,1)S(1)}, u32[]{:S(2)}, u32[]{:S(2)}) async-start(bf16[16,64,128]{2,1,0:T(8,128)(2,1)} %bitcast.16), calls=%async_computation | async-start | bytes 524288 | tf_op jit(solution)/shard_map/all_to_all | solution.py:28
  177.0 0.8 dynamic_slice.7
  177.7 8.9 %all-to-all-done = bf16[16,64,128]{2,1,0:T(8,128)(2,1)S(1)} async-done(((bf16[16,64,128]{2,1,0:T(8,128)(2,1)}), bf16[16,64,128]{2,1,0:T(8,128)(2,1)S(1)}, u32[]{:S(2)}, u32[]{:S(2)}) %all-to-all-start) | async-done | bytes 262176 | tf_op jit(solution)/shard_map/all_to_all | solution.py:28
  186.7 4.9 %all-gather.11.cloned.1.call-done = bf16[4096,128]{1,0:T(8,128)(2,1)} async-done(((bf16[1024,128]{1,0:T(8,128)(2,1)}), bf16[4096,128]{1,0:T(8,128)(2,1)}) %all-gather.11.cloned.1.call-update) | async-done | bytes 1048592 | tf_op jit(solution)/shard_map/all_gather | solution.py:16
  191.6 1.8 fusion.14
  193.9 16.6 %all_to_all.11 = f32[16,1,64]{2,1,0:T(1,128)S(1)} all-to-all(f32[16,1,64]{2,1,0:T(1,128)S(1)} %broadcast_in_dim.15), channel_id=1, replica_groups=mesh['batch_0'=4,'batch_1'=4,'field'=2,'dim'=8] {'field','dim'}, dimensions={0} | all-to-all | bytes 8192 | tf_op jit(solution)/shard_map/all_to_all | solution.py:40
  210.5 0.5 broadcast.18
  211.0 0.7 reduce.7
  211.7 0.7 reshape.64
  (33 shorter events, 2.0 us)
Async XLA Ops:
  7.2 160.0 %copy-start = (bf16[64,128]{1,0:T(8,128)(2,1)S(1)}, bf16[64,128]{1,0:T(8,128)(2,1)}, u32[]{:S(2)}) copy-start(bf16[64,128]{1,0:T(8,128)(2,1)} %param.14) | copy-start | bytes 49156
  7.2 54.4 %all-gather.5.cloned.1.call-start = ((), (), s32[]{:S(2)}) async-start(), calls=%async_computation.2 | async-start | bytes 7241728 | tf_op jit(solution)/shard_map/all_gather | solution.py:65
  7.9 106.4 %all-gather.7.cloned.1.call-start = ((), (), s32[]{:S(2)}) async-start(), calls=%async_computation.3 | async-start | bytes 7241728 | tf_op jit(solution)/shard_map/all_gather | solution.py:65
  19.1 10.9 %copy-start.5 = (f32[2,13,16]{2,0,1:T(2,128)S(1)}, f32[2,13,16]{2,0,1:T(2,128)}, u32[]{:S(2)}) copy-start(f32[2,13,16]{2,0,1:T(2,128)} %param.11) | copy-start | bytes 4996
  61.6 4.6 %copy-start.1 = (bf16[13,16,1024]{2,1,0:T(8,128)(2,1)S(1)}, bf16[13,16,1024]{2,1,0:T(8,128)(2,1)}, u32[]{:S(2)}) copy-start(bf16[13,16,1024]{2,1,0:T(8,128)(2,1)} %param.9) | copy-start | bytes 1277956
  67.1 100.0 %all-gather.9.cloned.1.call-start = ((), (), s32[]{:S(2)}) async-start(), calls=%async_computation.4 | async-start | bytes 7241728 | tf_op jit(solution)/shard_map/all_gather | solution.py:124
  114.3 4.7 %copy-start.2 = (bf16[13,16,1024]{2,1,0:T(8,128)(2,1)S(1)}, bf16[13,16,1024]{2,1,0:T(8,128)(2,1)}, u32[]{:S(2)}) copy-start(bf16[13,16,1024]{2,1,0:T(8,128)(2,1)} %fusion.7) | copy-start | bytes 1277956
  114.3 5.7 %copy-start.4 = (bf16[256,128]{1,0:T(8,128)(2,1)S(1)}, bf16[256,128]{1,0:T(8,128)(2,1)}, u32[]{:S(2)}) copy-start(bf16[256,128]{1,0:T(8,128)(2,1)} %param.16) | copy-start | bytes 196612
  118.9 11.2 %copy-start.3 = (bf16[64,26,128]{2,0,1:T(8,128)(2,1)S(1)}, bf16[64,26,128]{2,0,1:T(8,128)(2,1)}, u32[]{:S(2)}) copy-start(bf16[64,26,128]{2,0,1:T(8,128)(2,1)} %param.12) | copy-start | bytes 1277956
  119.0 48.2 %copy-start.6 = (f32[64]{0:T(128)S(1)}, f32[64]{0:T(128)}, u32[]{:S(2)}) copy-start(f32[64]{0:T(128)} %param.13) | copy-start | bytes 772
  120.0 71.6 %all-gather.11.cloned.1.call-start = ((), (), s32[]{:S(2)}) async-start(), calls=%async_computation.5 | async-start | bytes 1310720 | tf_op jit(solution)/shard_map/all_gather | solution.py:16
  172.4 14.2 %all-to-all-start = ((bf16[16,64,128]{2,1,0:T(8,128)(2,1)}), bf16[16,64,128]{2,1,0:T(8,128)(2,1)S(1)}, u32[]{:S(2)}, u32[]{:S(2)}) async-start(bf16[16,64,128]{2,1,0:T(8,128)(2,1)} %bitcast.16), calls=%async_computation | async-start | bytes 524288 | tf_op jit(solution)/shard_map/all_to_all | solution.py:28
Sparse Core Ops, SparseCore 0:
  9.8 51.7 all-gather.4
  67.2 46.9 all-gather.6
  120.1 46.9 all-gather.8
  168.8 22.7 all-gather.10
where the time goes:
time: 220 us; the launch traced here: 219 us
  waiting for transfers between devices  109 us (50%)
  local copies, waits for them, and re-layouts  44.8 us (20%)
  blocking collectives  26.7 us (12%)
  matrix products  16.3 us (7%)
  between operations  13.9 us (6%)
  starting transfers between devices  4.74 us (2%)
  other arithmetic  3.03 us (1%)
    all_gather x2, waiting for transfers between devices, cross_flat(): lax.all_gather(flattened, ('field', 'dim'), axis=0, tiled=True)  58.5 us
    all_gather x1, waiting for transfers between devices, body(): lax.all_gather(flattened, ('field', 'dim'), axis=0, tiled=True)  36.4 us
    transpose x3, local copies, waits for them, and re-layouts, by_device(): shaped = shaped.transpose(1, 3, 0, 2, 4)  22.1 us
    another operation x2, local copies, waits for them, and re-layouts, by_device(): weights.reshape(out_count, field_count, fields_all // field_count, dim_co...  17.4 us
    all_to_all x1, blocking collectives, sent_to_all(): return lax.all_to_all(copies, axis, split_axis=0, concat_axis=0, tiled=True)  16.6 us
    all_gather x1, blocking collectives, whole_of(): nearer = lax.all_gather(x, axes[-1], axis=dim, tiled=True)  10.1 us
    dot_general x2, matrix products, row_adder(): jnp.einsum('kib,koi->ob', shards, blocks, preferred_element_type=jnp.floa...  9.24 us
    all_to_all x1, waiting for transfers between devices, summed_on_arrival(): pieces = lax.all_to_all(cut_along(x, dim, length), axis, 0, 0, tiled=True)  8.89 us
  transfers between devices with their start and end apart: 5, of which 5 were waited for; matrix products, arithmetic and copies ran while one was open for 22% of the time, Pallas kernels for 0%

commit v1 on v0

v1 whole, which is shorter than its diff:
```python
import functools
import math

import jax
import jax.numpy as jnp
from jax import lax
from jax.experimental import pallas as pl
from jax.experimental.pallas import tpu as pltpu
from jax.sharding import Mesh
from jax.sharding import PartitionSpec as P

BATCH = ("batch_0", "batch_1")
MESH = pl.DeviceIdType.MESH
F32 = jnp.float32
BF16 = jnp.bfloat16

FIELDS = 26
NX = 4
NZ = 8
HALF = 13
SUB = 16
BLK = 7
NY = 6
NREST = FIELDS + 1 - NX * NY
KB = FIELDS + 1
KA = NY * 128
KR = NREST * 128
KW = KB * 128
QUART = 52
TC = BLK * 128 + 256
UNITS = 1024


def copy(src, dst, send, recv, where):
    return pltpu.make_async_remote_copy(
        src_ref=src, dst_ref=dst, send_sem=send, recv_sem=recv, device_id=where, device_id_type=MESH
    )


def arrived(ref, sem):
    pltpu.make_async_copy(ref, ref, sem).wait()


def slot_shift(s):
    return jnp.where(s % 2 == 1, (s + 1) // 2, (NZ - s // 2) % NZ)


def kernel(
    feat, w_own, t_own, c_own, user_t, target,
    out, loss,
    a1, a2, w, t, cur1, cur2, part, mine, rs, cands, logits,
    a2a_s, a2a_r, ag1_s, ag1_r, ag1_ls, ag2_s, ag2_r, ag2_ls, ag2_lr,
    z_s, z_r, y_s, y_r, l_s, l_r, d_s, d_r,
    t_s, t_r, td_s, td_r, c_s, c_r, rs_s, rs_r, o_s, o_r, g_s, g_r,
):
    x = lax.axis_index("batch_1")
    y = lax.axis_index("batch_0")
    z = lax.axis_index("dim")
    c = lax.axis_index("field")
    p = x % 2
    wide = x // 2
    tall = 1 - wide
    xr, xl = (x + 1) % NX, (x + NX - 1) % NX
    yr, yl = (y + 1) % NX, (y + NX - 1) % NX
    zr, zl = (z + 1) % NZ, (z + NZ - 1) % NZ
    first = 2 * (1 - c)

    def lanes(j):
        return pl.ds(pl.multiple_of(j * 128, 128), 128)

    def ycols(who):
        return pl.ds(pl.multiple_of(who * KA, 128), KA)

    rest = pl.ds(NX * NY * 128, KR)

    @pl.loop(1, NZ)
    def _(dz):
        to = (z + dz) % NZ
        copy(
            feat.at[:, :, lanes(to)],
            a1.at[pl.ds(HALF * c, HALF), z, :, lanes(p)],
            a2a_s.at[0], a2a_r.at[dz], {"dim": to, "field": tall},
        ).start()

    @pl.when(c == wide)
    def _():
        copy(
            feat.at[:, :, lanes(z)],
            a1.at[pl.ds(HALF * c, HALF), z, :, lanes(p)],
            a2a_s.at[1], a2a_r.at[0], {"field": tall},
        ).start()

    @pl.when(c == tall)
    def _():
        a1[pl.ds(HALF * c, HALF), z, :, lanes(p)] = feat[:, :, lanes(z)]
        cands[NX * y + x] = c_own[...]
        for step in range(1, NX):
            to = (x + step) % NX
            copy(
                c_own, cands.at[NX * y + x], c_s.at[0], c_r.at[0], {"batch_1": to, "field": 1 - to // 2}
            ).start()

    row = lax.broadcasted_iota(jnp.int32, (NZ, SUB, 256), 0) * SUB + lax.broadcasted_iota(
        jnp.int32, (NZ, SUB, 256), 1
    )
    ones = jnp.where(row < 3, 1.0, 0.0).astype(BF16)
    a1[FIELDS] = ones
    a2[FIELDS * NZ : KB * NZ] = ones
    t[z, c] = t_own[...]

    def from_z(level, s):
        src = (z + NZ - slot_shift(s)) % NZ
        own = w.at[level, :, src, :, ycols(y)]
        tail = w.at[level, :, src, :, rest]

        def on(ref, k, d):
            to = jnp.where(d == 0, zr, zl)
            nxt = jnp.where(s == 0, 1 + d, jnp.minimum(s + 2, NZ - 1))
            copy(ref, ref, z_s.at[level, d, k], z_r.at[level, nxt, k], {"dim": to}).start()

        d = jnp.where(s % 2 == 1, 0, 1)

        @pl.when(s > 0)
        def _():
            arrived(own, z_r.at[level, s, 0])

        @pl.when((s > 0) & (s < 6))
        def _():
            on(own, 0, d)

        @pl.when(s == 0)
        def _():
            on(own, 0, 0)
            on(own, 0, 1)

        copy(own, own, y_s.at[level, 0], y_r.at[level, s, 0], {"batch_0": yr}).start()
        copy(own, own, y_s.at[level, 1], y_r.at[level, s, 1], {"batch_0": yl}).start()

        @pl.when(s > 0)
        def _():
            arrived(tail, z_r.at[level, s, 1])

        @pl.when((s > 0) & ((s < 5) | (s == 6)))
        def _():
            on(tail, 1, d)

        @pl.when(s == 0)
        def _():
            on(tail, 1, 0)
            on(tail, 1, 1)

    def from_y(level, s):
        src = (z + NZ - slot_shift(s)) % NZ
        left = w.at[level, :, src, :, ycols(yl)]
        right = w.at[level, :, src, :, ycols(yr)]
        arrived(left, y_r.at[level, s, 0])
        up = w.at[level, pl.ds(0, 4), src, :, ycols(yl)]
        copy(up, up, l_s.at[level, 0], l_r.at[level, s, 0], {"batch_0": yr}).start()
        arrived(right, y_r.at[level, s, 1])
        down = w.at[level, pl.ds(4, 3), src, :, ycols(yr)]
        copy(down, down, l_s.at[level, 1], l_r.at[level, s, 1], {"batch_0": yl}).start()

    def to_core(level, s):
        src = (z + NZ - slot_shift(s)) % NZ
        far = (y + 2) % NX
        arrived(w.at[level, pl.ds(0, 4), src, :, ycols(far)], l_r.at[level, s, 0])
        arrived(w.at[level, pl.ds(4, 3), src, :, ycols(far)], l_r.at[level, s, 1])
        piece = w.at[level, :, src]
        copy(piece, piece, d_s.at[level], d_r.at[level], {"field": 1 - c}).start()

    def tower_step(s):
        src = (z + NZ - slot_shift(s)) % NZ
        whole = t.at[src, c]

        @pl.when(s == 0)
        def _():
            copy(whole, whole, t_s.at[0], t_r.at[1], {"dim": zr}).start()
            copy(whole, whole, t_s.at[1], t_r.at[2], {"dim": zl}).start()

        @pl.when((s > 0) & (s < 7))
        def _():
            arrived(whole, t_r.at[s])

        for par, to in ((1, zr), (0, zl)):
            d = 1 - par
            half = t.at[src, c, pl.ds(32 * d, 32)]

            @pl.when((s > 0) & (s < 5) & (s % 2 == par))
            def _():
                copy(whole, whole, t_s.at[d], t_r.at[s + 2], {"dim": to}).start()

            @pl.when(s == 6 - par)
            def _():
                copy(half, half, t_s.at[2 + d], t_r.at[7 + d], {"dim": to}).start()

        @pl.when(s == 7)
        def _():
            arrived(t.at[src, c, pl.ds(0, 32)], t_r.at[7])
            arrived(t.at[src, c, pl.ds(32, 32)], t_r.at[8])

        copy(whole, whole, td_s, td_r, {"field": 1 - c}).start()

    def example_step(s):
        dz = slot_shift(s)
        src = (z + NZ - dz) % NZ
        whole = a1.at[pl.ds(0, FIELDS), src, :, lanes(p)]

        @pl.when(s == 0)
        def _():
            arrived(a1.at[pl.ds(0, HALF), src, :, lanes(p)], a2a_r.at[0])

        @pl.when(s > 0)
        def _():
            arrived(whole, a2a_r.at[dz])

        copy(whole, whole, ag1_s.at[0], ag1_r.at[p, s, 0], {"batch_1": xr}).start()
        copy(whole, whole, ag1_s.at[1], ag1_r.at[p, s, 1], {"batch_1": xl}).start()

    def relay_step(s):
        src = (z + NZ - slot_shift(s)) % NZ
        for j in range(2):
            r = (x + NX - first - j) % NX
            whole = a1.at[pl.ds(0, FIELDS), src, :, pl.ds(128 * j, 128)]

            @pl.when(r == 1)
            def _():
                arrived(whole, ag1_r.at[j, s, 0])
                half = a1.at[pl.ds(0, HALF), src, :, pl.ds(128 * j, 128)]
                copy(half, half, ag1_ls.at[0], ag1_r.at[j, s, 0], {"batch_1": xr}).start()

            @pl.when(r == 3)
            def _():
                arrived(whole, ag1_r.at[j, s, 1])
                half = a1.at[pl.ds(HALF, HALF), src, :, pl.ds(128 * j, 128)]
                copy(half, half, ag1_ls.at[1], ag1_r.at[j, s, 1], {"batch_1": xl}).start()

    def far_step(s):
        src = (z + NZ - slot_shift(s)) % NZ
        for j in range(2):
            r = (x + NX - first - j) % NX

            @pl.when(r == 2)
            def _():
                arrived(a1.at[pl.ds(0, HALF), src, :, pl.ds(128 * j, 128)], ag1_r.at[j, s, 0])
                arrived(a1.at[pl.ds(HALF, HALF), src, :, pl.ds(128 * j, 128)], ag1_r.at[j, s, 1])

    def tiles(who, h):
        return a2.at[pl.ds(QUART * who + 26 * h, 26)]

    def second_send():
        for h in range(2):
            mineh = cur1.at[pl.ds(4 * p + 26 * h, 26)]
            copy(mineh, tiles(x, h), ag2_s.at[h, 0], ag2_r.at[h, 0], {"batch_1": xr}).start()
            copy(mineh, tiles(x, h), ag2_s.at[h, 1], ag2_r.at[h, 1], {"batch_1": xl}).start()

    def second_step(h):
        for d in ((0, 1) if h == 0 else (1, 0)):
            who, to = ((xl, xr), (xr, xl))[d]
            arrived(tiles(who, h), ag2_r.at[h, d])
            if d == h:
                copy(tiles(who, h), tiles(who, h), ag2_ls.at[h], ag2_lr.at[h], {"batch_1": to}).start()

    def second_far():
        far = (x + 2) % NX
        arrived(tiles(far, 0), ag2_lr.at[0])
        arrived(tiles(far, 1), ag2_lr.at[1])

    @pl.when(c == wide)
    def _():
        w[:, :, z, :, ycols(y)] = w_own[:, :, :, 0:KA]
        w[:, :, z, :, NX * NY * 128 :] = w_own[:, :, :, KA:]

        @pl.loop(0, NZ + 2)
        def _(i):
            @pl.when(i < NZ)
            def _():
                from_z(0, i)

            @pl.when((i > 0) & (i < NZ + 1))
            def _():
                from_y(0, i - 1)

            @pl.when(i > 1)
            def _():
                to_core(0, i - 2)

            @pl.when(i < NZ)
            def _():
                relay_step(i)

        from_z(1, 0)

        @pl.loop(0, NZ)
        def _(i):
            far_step(i)

    @pl.when(c == tall)
    def _():
        @pl.loop(0, NZ)
        def _(i):
            example_step(i)
            relay_step(i)

        tower_step(0)
        arrived(w.at[0], d_r.at[0])

    base = HALF * wide + 6 * p

    @pl.loop(0, BLK)
    def _(f):
        lhs = w[0, f].reshape(128, KW)
        prod = jnp.dot(lhs, a1[...].reshape(KW, 256), preferred_element_type=F32)
        anchor = a1[base + f].reshape(128, 256).astype(F32)
        nxt = (anchor * prod + anchor).astype(BF16)
        cur1[pl.ds(NZ * f, NZ)] = nxt.reshape(NZ, SUB, 256)

    second_send()
    a2[pl.ds(QUART * x, QUART)] = cur1[pl.ds(4 * p, QUART)]

    @pl.when(c == wide)
    def _():
        tower_step(0)

        @pl.loop(1, NZ + 2)
        def _(i):
            @pl.when(i < NZ)
            def _():
                from_z(1, i)

            from_y_ok = i < NZ + 1

            @pl.when(from_y_ok)
            def _():
                from_y(1, i - 1)

            @pl.when(i > 1)
            def _():
                to_core(1, i - 2)

            @pl.when(i < NZ)
            def _():
                tower_step(i)

            @pl.when(i == 3)
            def _():
                second_step(0)

            @pl.when(i == 6)
            def _():
                second_step(1)

        second_far()

    @pl.when(c == tall)
    def _():
        got = cands.at[pl.ds(NX * y, NX)]
        arrived(cands.at[pl.ds(NX * y, NX - 1)], c_r.at[0])
        for step in range(1, NX):
            copy(got, got, c_s.at[1], c_r.at[1], {"batch_0": (y + step) % NX}).start()

        @pl.loop(1, NZ)
        def _(i):
            tower_step(i)

            @pl.when(i == 3)
            def _():
                second_step(0)

            @pl.when(i == 5)
            def _():
                second_step(1)

        second_far()
        arrived(w.at[1], d_r.at[1])

    @pl.loop(0, BLK)
    def _(f):
        lhs = w[1, f].reshape(128, KW)
        prod = jnp.dot(lhs, a2[...].reshape(KW, 256), preferred_element_type=F32)
        anchor = a1[base + f].reshape(128, 256).astype(F32)
        before = cur1[pl.ds(NZ * f, NZ)].reshape(128, 256).astype(F32)
        nxt = (anchor * prod + before).astype(BF16)
        cur2[f] = nxt.reshape(NZ, SUB, 256)

    arrived(t.at[:, c], td_r)

    @pl.loop(0, NZ)
    def _(k):
        lhs = t[k, :, :, 0 : BLK * 128].reshape(128, BLK * 128)
        prod = jnp.dot(lhs, cur2[...].reshape(BLK * 128, 256), preferred_element_type=F32)
        part[pl.ds(128 * k, 128)] = prod.astype(BF16)
        mine[pl.ds(128 * k, 128)] = prod

    for j in range(2):
        @pl.when(x != first + j)
        def _():
            r = (x + NX - first - j) % NX
            copy(
                part.at[:, pl.ds(128 * j, 128)], rs.at[r - 1], rs_s.at[j], rs_r, {"batch_1": first + j}
            ).start()

    @pl.loop(0, 2 * NZ)
    def _(i):
        j, to = i // NZ, i % NZ
        where = {"batch_1": first + j, "dim": to, "field": wide}
        copy(
            cur2.at[pl.ds(p, 6), to, :, lanes(j)],
            out.at[pl.ds(7 * p, 6), :, lanes(z)],
            o_s.at[0], o_r, where,
        ).start()

        @pl.when((to // 4) == p)
        def _():
            copy(
                cur2.at[pl.ds(6 - 6 * p, 1), to, :, lanes(j)],
                out.at[pl.ds(6, 1), :, lanes(z)],
                o_s.at[1], o_r, where,
            ).start()

    @pl.when(c == tall)
    def _():
        arrived(rs, rs_r)
        here = lanes(p)
        bias = t[:, :, :, BLK * 128 + 128 :].reshape(UNITS, 128).astype(F32)
        bias = bias[:, 0:1] + bias[:, 1:2] + bias[:, 2:3]
        total = mine[:, here] + rs[0].astype(F32) + rs[1].astype(F32) + rs[2].astype(F32)
        hidden = jnp.maximum(total + bias, 0.0).astype(BF16)
        qw = t[:, :, :, BLK * 128 : BLK * 128 + 128].reshape(UNITS, 128)
        query = lax.dot_general(qw, hidden, (((0,), (0,)), ((), ())), preferred_element_type=F32)
        query = (query + user_t[...].astype(F32)).astype(BF16)

        arrived(cands.at[pl.ds(0, 3 * NX)], c_r.at[1])
        scale = 1.0 / math.sqrt(128)

        def scores(k, top):
            got = jnp.dot(cands[k], query, preferred_element_type=F32) * scale
            logits[k] = got
            return jnp.maximum(top, jnp.max(got.reshape(32, 8, 128), axis=0))

        top = lax.fori_loop(0, NX * NX, scores, jnp.full((8, 128), -1e30, F32))
        top = jnp.max(top, axis=0, keepdims=True)
        wanted = target[0:1, :]
        index = lax.broadcasted_iota(jnp.int32, (256, 128), 0)

        def sums(k, carry):
            total, picked = carry
            got = logits[k]
            e = jnp.exp(got - top)
            hit = jnp.where(index == wanted - 256 * k, got, 0.0)
            return (
                total + jnp.sum(e.reshape(32, 8, 128), axis=0),
                picked + jnp.sum(hit.reshape(32, 8, 128), axis=0),
            )

        zero = jnp.zeros((8, 128), F32)
        total, picked = lax.fori_loop(0, NX * NX, sums, (zero, zero))
        total = jnp.sum(total, axis=0, keepdims=True)
        picked = jnp.sum(picked, axis=0, keepdims=True)
        result = top + jnp.log(total) - picked
        loss[z] = jnp.broadcast_to(result, (8, 128))

        @pl.loop(1, NZ)
        def _(dz):
            to = (z + dz) % NZ
            copy(loss.at[z], loss.at[z], g_s.at[0], g_r, {"dim": to}).start()
            copy(loss.at[z], loss.at[z], g_s.at[1], g_r, {"dim": to, "field": wide}).start()

        copy(loss.at[z], loss.at[z], g_s.at[2], g_r, {"field": wide}).start()
        arrived(loss.at[pl.ds(0, NZ - 1)], g_r)
        arrived(loss.at[pl.ds(0, NZ - 1)], g_s.at[0])
        arrived(loss.at[pl.ds(0, NZ - 1)], g_s.at[1])
        arrived(loss.at[0], g_s.at[2])
        arrived(cands.at[pl.ds(0, 3)], c_s.at[0])
        arrived(cands.at[pl.ds(0, 3 * NX)], c_s.at[1])
        for d in range(2):
            arrived(a1.at[pl.ds(0, FIELDS), :, :, pl.ds(0, 128)], ag1_s.at[d])

    @pl.when(c == wide)
    def _():
        arrived(loss, g_r)
        arrived(feat.at[:, :, pl.ds(0, 128)], a2a_s.at[1])
        for level in range(2):
            arrived(w.at[level, :, pl.ds(0, 4), :, pl.ds(0, KA)], z_s.at[level, 0, 0])
            arrived(w.at[level, :, pl.ds(0, 3), :, pl.ds(0, KA)], z_s.at[level, 1, 0])
            arrived(w.at[level, :, pl.ds(0, 3), :, rest], z_s.at[level, 0, 1])
            arrived(w.at[level, :, pl.ds(0, 4), :, rest], z_s.at[level, 1, 1])
            arrived(w.at[level, :, :, :, pl.ds(0, KA)], y_s.at[level, 0])
            arrived(w.at[level, :, :, :, pl.ds(0, KA)], y_s.at[level, 1])
            arrived(w.at[level, pl.ds(0, 4), :, :, pl.ds(0, KA)], l_s.at[level, 0])
            arrived(w.at[level, pl.ds(4, 3), :, :, pl.ds(0, KA)], l_s.at[level, 1])
            arrived(w.at[level], d_s.at[level])

    arrived(feat.at[:, :, pl.ds(0, 128 * (NZ - 1))], a2a_s.at[0])
    for j in range(2):
        r = (x + NX - first - j) % NX

        @pl.when(r == 1)
        def _():
            arrived(a1.at[pl.ds(0, HALF), :, :, pl.ds(0, 128)], ag1_ls.at[0])

        @pl.when(r == 3)
        def _():
            arrived(a1.at[pl.ds(0, HALF), :, :, pl.ds(0, 128)], ag1_ls.at[1])

        @pl.when(r != 0)
        def _():
            arrived(rs.at[0], rs_s.at[j])

    for h in range(2):
        for d in range(2):
            arrived(tiles(0, h), ag2_s.at[h, d])
        arrived(tiles(0, h), ag2_ls.at[h])
    for d in range(2):
        arrived(t.at[pl.ds(0, 3), 0], t_s.at[d])
        arrived(t.at[0, 0, pl.ds(0, 32)], t_s.at[2 + d])
    arrived(t.at[:, 0], td_s)
    arrived(cur2.at[pl.ds(0, 6)], o_s.at[0])
    arrived(cur2.at[0, pl.ds(0, 4)], o_s.at[1])
    arrived(out, o_r)


def three_parts(v):
    hi = lax.reduce_precision(v, 8, 7)
    mid = lax.reduce_precision(v - hi, 8, 7)
    low = (v - hi) - mid
    return jnp.stack([hi, mid, low], axis=-1).astype(BF16)


def lane_block(parts):
    return jnp.pad(parts, [(0, 0)] * (parts.ndim - 1) + [(0, 128 - parts.shape[-1])])


def body(features, cross_weight, cross_bias, tower_weight, tower_bias, query_weight, user_vec, candidates, positive):
    x = lax.axis_index("batch_1")
    y = lax.axis_index("batch_0")
    z = lax.axis_index("dim")
    p = x % 2

    rows = lax.dynamic_slice_in_dim(cross_weight, 6 * p, BLK, 1)
    own = lax.dynamic_slice_in_dim(rows, NY * y, NY, 3)
    rest = rows[:, :, :, NX * NY :]
    bias = lane_block(three_parts(lax.dynamic_slice_in_dim(cross_bias, 6 * p, BLK, 1)))
    w_own = jnp.concatenate([own, rest, bias[:, :, :, None]], axis=3).reshape(2, BLK, SUB, KA + KR)

    cols = lax.dynamic_slice_in_dim(tower_weight, (13 * x) // 2, BLK, 1).reshape(64, BLK * 128)
    at = lax.broadcasted_iota(jnp.int32, (1, BLK * 128), 1) - 64 * p
    cols = jnp.where((at >= 0) & (at < 832), cols, jnp.zeros_like(cols))
    t_own = jnp.concatenate([cols, query_weight, lane_block(three_parts(tower_bias))], axis=1)

    user_t = lax.dynamic_slice_in_dim(user_vec, 128 * z, 128, 0).T
    target = jnp.broadcast_to(lax.dynamic_slice_in_dim(positive, 128 * z, 128, 0)[None], (8, 128))

    vmem = pl.BlockSpec(memory_space=pltpu.VMEM)
    dma = pltpu.SemaphoreType.DMA
    out, loss = pl.pallas_call(
        kernel,
        out_shape=(
            jax.ShapeDtypeStruct((HALF, SUB, 1024), BF16),
            jax.ShapeDtypeStruct((NZ, 8, 128), F32),
        ),
        in_specs=[vmem] * 6,
        out_specs=(vmem, vmem),
        scratch_shapes=[
            pltpu.VMEM((KB, NZ, SUB, 256), BF16),
            pltpu.VMEM((KB * NZ, SUB, 256), BF16),
            pltpu.VMEM((2, BLK, NZ, SUB, KW), BF16),
            pltpu.VMEM((NZ, 2, 64, TC), BF16),
            pltpu.VMEM((BLK * NZ, SUB, 256), BF16),
            pltpu.VMEM((BLK, NZ, SUB, 256), BF16),
            pltpu.VMEM((UNITS, 256), BF16),
            pltpu.VMEM((UNITS, 256), F32),
            pltpu.VMEM((3, UNITS, 128), BF16),
            pltpu.VMEM((NX * NX, 256, 128), BF16),
            pltpu.VMEM((NX * NX, 256, 128), F32),
            dma((2,)), dma((NZ,)),
            dma((2,)), dma((2, NZ, 2)), dma((2,)),
            dma((2, 2)), dma((2, 2)), dma((2,)), dma((2,)),
            dma((2, 2, 2)), dma((2, NZ, 2)),
            dma((2, 2)), dma((2, NZ, 2)),
            dma((2, 2)), dma((2, NZ, 2)),
            dma((2,)), dma((2,)),
            dma((4,)), dma((9,)), dma, dma,
            dma((2,)), dma((2,)),
            dma((2,)), dma,
            dma((2,)), dma,
            dma((3,)), dma,
        ],
        compiler_params=pltpu.CompilerParams(has_side_effects=True, vmem_limit_bytes=60 * 1024 * 1024),
        name="dcn",
    )(features, w_own, t_own, candidates, user_t, target)
    return out, loss[:, 0, :].reshape(1024)


def solution(mesh):
    torus = Mesh(
        mesh.devices.reshape(4, 4, mesh.shape["field"], mesh.shape["dim"]),
        ("batch_0", "batch_1", "field", "dim"),
    )
    in_specs = (
        P("field", "dim", BATCH),
        P(None, "field", "dim", None, None),
        P(None, "field", "dim"),
        P(("field", "dim"), None, None),
        P(("field", "dim")),
        P(("field", "dim"), None),
        P(BATCH, None),
        P(BATCH, None),
        P(BATCH),
    )
    out_specs = (P("field", "dim", BATCH), P(BATCH))
    return jax.shard_map(body, mesh=torus, in_specs=in_specs, out_specs=out_specs, check_vma=False)
```

time: 220 us -> 136 us (0.62)
  Pallas kernels: 0 us -> 125 us
  waiting for transfers between devices: 109 us -> 0 us
  local copies, waits for them, and re-layouts: 44.8 us -> 6.76 us
  blocking collectives: 26.7 us -> 0 us
  matrix products: 16.3 us -> 0 us
  between operations: 13.9 us -> 0.75 us
  starting transfers between devices: 4.74 us -> 0 us
    pallas_call x0 -> x1, Pallas kernels: none -> 125 us  [body(): pl.pallas_call(kernel, out_shape=(jax.ShapeDtypeStruct((HALF, SUB, 1024),...]
    all_gather x4 -> x0, waiting for transfers between devices: 99.8 us -> none  [the longest x2 58.5 us: cross_flat(): lax.all_gather(flattened, ('field', 'dim'), axis=0, tiled=True)]
    transpose x3 -> x0, local copies, waits for them, and re-layouts: 22.1 us -> none  [by_device(): shaped = shaped.transpose(1, 3, 0, 2, 4)]
    another operation x2 -> x1, local copies, waits for them, and re-layouts: 17.4 us -> 0.11 us  [three_parts(): return jnp.stack([hi, mid, low], axis=-1).astype(BF16)]
    all_to_all x1 -> x0, blocking collectives: 16.6 us -> none  [sent_to_all(): return lax.all_to_all(copies, axis, split_axis=0, concat_axis=0, tiled=True)]
    dot_general x4 -> x0, matrix products: 16.3 us -> none  [the longest x2 9.24 us: row_adder(): jnp.einsum('kib,koi->ob', shards, blocks, preferred_element_type=jnp.floa...]
    all_gather x1 -> x0, blocking collectives: 10.1 us -> none  [whole_of(): nearer = lax.all_gather(x, axes[-1], axis=dim, tiled=True)]
    all_to_all x1 -> x0, waiting for transfers between devices: 8.89 us -> none  [summed_on_arrival(): pieces = lax.all_to_all(cut_along(x, dim, length), axis, 0, 0, tiled=True)]
  transfers between devices with their start and end apart: 5 -> 0, of which waited for: 5 -> 0; matrix products, arithmetic and copies ran while one was open for 22% -> 0% of each run, Pallas kernels for 0% -> 0%
where the time goes in v1:
time: 136 us
  Pallas kernels  125 us (92%)
  local copies, waits for them, and re-layouts  6.76 us (5%)
  other arithmetic  3.55 us (3%)
    pallas_call x1, Pallas kernels, body(): pl.pallas_call(kernel, out_shape=(jax.ShapeDtypeStruct((HALF, SUB, 1024),...  125 us

profile of v1, /device:TPU:7, one launch (start us, length us, event | category | flops | bytes accessed | tf_op | source)
XLA Modules:
  0.0 135.9 jit_solution(16867954688019084207)
XLA Ops:
  0.6 0.0 copy-start
  0.6 0.0 copy-start.2
  0.7 0.0 copy-start.1
  0.7 0.9 fusion.13
  1.5 0.2 fusion.5
  1.8 0.5 copy.25
  2.4 0.1 copy-done
  2.5 0.8 copy_bitcast_fusion.w_own
  3.3 0.9 bitcast_select_fusion
  4.2 0.0 copy-done.2
  4.3 0.1 copy.28
  4.4 0.0 copy-done.1
  4.4 0.7 fusion.7.t_own
  5.1 0.8 constant_dynamic-slice_fusion
  5.8 0.7 copy.30
  6.6 0.8 dynamic_slice.24
  7.3 0.6 broadcast_in_dim.23.target
  7.9 124.8 %dcn.1 = (bf16[13,16,1024]{2,1,0:T(8,128)(2,1)}, f32[8,8,128]{2,1,0:T(8,128)}) custom-call(bf16[13,16,1024]{2,1,0:T(8,128)(2,1)} %feat.1, bf16[2,7,16,1152]{3,2,1,0:T(8,128)(2,1)} %copy_bitcast_fusion.w_own, bf16[64,1152]{1,0:T(8,128)(2,1)} %fusion.7.t_own, bf16[256,128]{1,0:T(8,128)(2,1)} %c_own.1, bf16[128,128]{1,0:T(8,128)(2,1)} %bitcast.26, ...), custom_call_target="tpu_custom_call" | custom-call | tf_op jit(solution)/shard_map/dcn/pallas_call | solution.py:555
  132.7 1.4 slice.7
  134.1 1.8 %copy.36 = bf16[13,16,1024]{2,1,0:T(8,128)(2,1)} copy(bf16[13,16,1024]{2,1,0:T(8,128)(2,1)} %get-tuple-element.14) | data formatting | bytes 851968
  (5 shorter events, 0.1 us)
Async XLA Ops:
  0.6 1.8 %copy-start = (bf16[2,13,16,26,128]{4,2,3,1,0:T(8,128)(2,1)S(1)}, bf16[2,13,16,26,128]{4,2,3,1,0:T(8,128)(2,1)}, u32[]{:S(2)}) copy-start(bf16[2,13,16,26,128]{4,2,3,1,0:T(8,128)(2,1)} %param.10) | copy-start | bytes 8306692
  0.6 3.6 %copy-start.2 = (f32[64]{0:T(128)S(1)}, f32[64]{0:T(128)}, u32[]{:S(2)}) copy-start(f32[64]{0:T(128)} %param.13) | copy-start | bytes 772
  0.7 3.7 %copy-start.1 = (bf16[64,128]{1,0:T(8,128)(2,1)S(1)}, bf16[64,128]{1,0:T(8,128)(2,1)}, u32[]{:S(2)}) copy-start(bf16[64,128]{1,0:T(8,128)(2,1)} %param.14) | copy-start | bytes 49156

commit v2 on v1

--- a/solution.py
+++ b/solution.py
@@ -46,12 +46,13 @@
 
 
 def kernel(
-    feat, w_own, t_own, c_own, user_t, target,
-    out, loss,
-    a1, a2, w, t, cur1, cur2, part, mine, rs, cands, logits,
+    feat, c_w, c_b, t_w, t_b, q_w, c_own, user, target,
+    out, loss_out,
+    a1, a2, w, t, cur1, cur2, part, mine, rs, hop, summed, cands, logits, u_own, loss,
+    w_l, t_l, u_l,
     a2a_s, a2a_r, ag1_s, ag1_r, ag1_ls, ag2_s, ag2_r, ag2_ls, ag2_lr,
-    z_s, z_r, y_s, y_r, l_s, l_r, d_s, d_r,
-    t_s, t_r, td_s, td_r, c_s, c_r, rs_s, rs_r, o_s, o_r, g_s, g_r,
+    z_s, z_r, y_s, y_r, l_s, l_r, da_s, da_r, db_s, db_r, dy_s, dy_r,
+    t_s, t_r, td_s, td_r, c_s, c_r, rs_s, rs_r, hop_r, o_s, o_r, g_s, g_r,
 ):
     x = lax.axis_index("batch_1")
     y = lax.axis_index("batch_0")
@@ -73,32 +74,46 @@
 
     rest = pl.ds(NX * NY * 128, KR)
 
-    @pl.loop(1, NZ)
-    def _(dz):
-        to = (z + dz) % NZ
-        copy(
-            feat.at[:, :, lanes(to)],
-            a1.at[pl.ds(HALF * c, HALF), z, :, lanes(p)],
-            a2a_s.at[0], a2a_r.at[dz], {"dim": to, "field": tall},
-        ).start()
+    barrier = pltpu.get_barrier_semaphore()
+
+    def greet(where):
+        pl.semaphore_signal(barrier, inc=1, device_id=where, device_id_type=MESH)
+
+    for step in range(1, NX):
+        for core in range(2):
+            greet({"batch_1": (x + step) % NX, "field": core})
+        greet({"batch_0": (y + step) % NX})
+    for step in range(1, NZ):
+        for core in range(2):
+            greet({"dim": (z + step) % NZ, "field": core})
+    greet({"field": 1 - c})
+
+    base = HALF * wide + 6 * p
+    own_w = [(level, k) for level in range(2) for k in range(NY + NREST - 1)]
+
+    def own_copy(level, k):
+        field = NY * y + k if k < NY else NX * NY + k - NY
+        return pltpu.make_async_copy(
+            c_w.at[level, pl.ds(6 * p, BLK), field], w.at[level, :, z, :, lanes(field)], w_l.at[level, k]
+        )
 
     @pl.when(c == wide)
     def _():
-        copy(
-            feat.at[:, :, lanes(z)],
-            a1.at[pl.ds(HALF * c, HALF), z, :, lanes(p)],
-            a2a_s.at[1], a2a_r.at[0], {"field": tall},
-        ).start()
+        for level, k in own_w:
+            own_copy(level, k).start()
+
+    t_copies = [
+        pltpu.make_async_copy(t_w.at[base + k], t.at[z, c, :, pl.ds(128 * k, 128)], t_l.at[k])
+        for k in range(BLK)
+    ]
+    for cp in t_copies:
+        cp.start()
+
+    u_copy = pltpu.make_async_copy(user.at[pl.ds(pl.multiple_of(128 * z, 128), 128)], u_own, u_l)
 
     @pl.when(c == tall)
     def _():
-        a1[pl.ds(HALF * c, HALF), z, :, lanes(p)] = feat[:, :, lanes(z)]
-        cands[NX * y + x] = c_own[...]
-        for step in range(1, NX):
-            to = (x + step) % NX
-            copy(
-                c_own, cands.at[NX * y + x], c_s.at[0], c_r.at[0], {"batch_1": to, "field": 1 - to // 2}
-            ).start()
+        u_copy.start()
 
     row = lax.broadcasted_iota(jnp.int32, (NZ, SUB, 256), 0) * SUB + lax.broadcasted_iota(
         jnp.int32, (NZ, SUB, 256), 1
@@ -106,67 +121,116 @@
     ones = jnp.where(row < 3, 1.0, 0.0).astype(BF16)
     a1[FIELDS] = ones
     a2[FIELDS * NZ : KB * NZ] = ones
-    t[z, c] = t_own[...]
-
-    def from_z(level, s):
+
+    def bias_block(values):
+        n = values.shape[1]
+        eye = lax.broadcasted_iota(jnp.int32, (n, n), 0) == lax.broadcasted_iota(jnp.int32, (n, n), 1)
+        col = jnp.sum(jnp.where(eye, values, 0.0), axis=1, keepdims=True)
+        hi = col.astype(BF16).astype(F32)
+        mid = (col - hi).astype(BF16).astype(F32)
+        low = (col - hi) - mid
+        lane = lax.broadcasted_iota(jnp.int32, (n, 128), 1)
+        terms = jnp.where(lane == 0, hi, jnp.where(lane == 1, mid, jnp.where(lane == 2, low, 0.0)))
+        return terms.astype(BF16)
+
+    t[z, c, :, BLK * 128 : BLK * 128 + 128] = q_w[...]
+    t[z, c, :, BLK * 128 + 128 :] = bias_block(t_b[...])
+
+    @pl.when(c == wide)
+    def _():
+        @pl.loop(0, BLK)
+        def _(f):
+            for level in range(2):
+                w[level, f, z, :, FIELDS * 128 :] = bias_block(c_b[6 * p + f, level : level + 1])
+
+        for level, k in own_w:
+            own_copy(level, k).wait()
+
+    @pl.when(c == tall)
+    def _():
+        a1[pl.ds(HALF * c, HALF), z, :, lanes(p)] = feat[:, :, lanes(z)]
+        cands[NX * y + x] = c_own[...]
+
+    for cp in t_copies:
+        cp.wait()
+    lane64 = lax.broadcasted_iota(jnp.int32, (64, 128), 1)
+    edge = lanes((BLK - 1) * (1 - p))
+    kept = (lane64 < 64) == (p == 0)
+    t[z, c, :, edge] = jnp.where(kept, t[z, c, :, edge].astype(F32), 0.0).astype(BF16)
+
+    pl.semaphore_wait(barrier, 3 * NX - 3 + 2 * NZ - 2 + 1)
+
+    def examples_out():
+        @pl.loop(1, NZ)
+        def _(s):
+            to = (z + slot_shift(s)) % NZ
+            copy(
+                feat.at[:, :, lanes(to)],
+                a1.at[pl.ds(HALF * c, HALF), z, :, lanes(p)],
+                a2a_s.at[0], a2a_r.at[slot_shift(s)], {"dim": to, "field": tall},
+            ).start()
+
+    def along_z(ref, level, s, k, d):
+        to = jnp.where(d == 0, zr, zl)
+        nxt = jnp.where(s == 0, 1 + d, jnp.minimum(s + 2, NZ - 1))
+        copy(ref, ref, z_s.at[level, d, k], z_r.at[level, nxt, k], {"dim": to}).start()
+
+    def from_z(level, s, k):
+        src = (z + NZ - slot_shift(s)) % NZ
+        ref = w.at[level, :, src, :, rest] if k else w.at[level, :, src, :, ycols(y)]
+        onward = ((s < 5) | (s == 6)) if k else (s < 6)
+
+        @pl.when(s > 0)
+        def _():
+            arrived(ref, z_r.at[level, s, k])
+
+        @pl.when((s > 0) & onward)
+        def _():
+            along_z(ref, level, s, k, jnp.where(s % 2 == 1, 0, 1))
+
+        @pl.when(s == 0)
+        def _():
+            along_z(ref, level, s, k, 0)
+            along_z(ref, level, s, k, 1)
+
+        if k:
+            copy(ref, ref, db_s.at[level], db_r.at[level], {"field": 1 - c}).start()
+        else:
+            copy(ref, ref, da_s.at[level], da_r.at[level, s], {"field": 1 - c}).start()
+
+    def from_a(level, s):
+        from_z(level, s, 0)
+
+    def from_b(level, s):
+        from_z(level, s, 1)
+
+    def to_y(level, s):
         src = (z + NZ - slot_shift(s)) % NZ
         own = w.at[level, :, src, :, ycols(y)]
-        tail = w.at[level, :, src, :, rest]
-
-        def on(ref, k, d):
-            to = jnp.where(d == 0, zr, zl)
-            nxt = jnp.where(s == 0, 1 + d, jnp.minimum(s + 2, NZ - 1))
-            copy(ref, ref, z_s.at[level, d, k], z_r.at[level, nxt, k], {"dim": to}).start()
-
-        d = jnp.where(s % 2 == 1, 0, 1)
-
-        @pl.when(s > 0)
-        def _():
-            arrived(own, z_r.at[level, s, 0])
-
-        @pl.when((s > 0) & (s < 6))
-        def _():
-            on(own, 0, d)
-
-        @pl.when(s == 0)
-        def _():
-            on(own, 0, 0)
-            on(own, 0, 1)
-
+        arrived(own, da_r.at[level, s])
         copy(own, own, y_s.at[level, 0], y_r.at[level, s, 0], {"batch_0": yr}).start()
         copy(own, own, y_s.at[level, 1], y_r.at[level, s, 1], {"batch_0": yl}).start()
-
-        @pl.when(s > 0)
-        def _():
-            arrived(tail, z_r.at[level, s, 1])
-
-        @pl.when((s > 0) & ((s < 5) | (s == 6)))
-        def _():
-            on(tail, 1, d)
-
-        @pl.when(s == 0)
-        def _():
-            on(tail, 1, 0)
-            on(tail, 1, 1)
 
     def from_y(level, s):
         src = (z + NZ - slot_shift(s)) % NZ
         left = w.at[level, :, src, :, ycols(yl)]
         right = w.at[level, :, src, :, ycols(yr)]
+        up = w.at[level, pl.ds(0, 4), src, :, ycols(yl)]
+        down = w.at[level, pl.ds(4, 3), src, :, ycols(yr)]
         arrived(left, y_r.at[level, s, 0])
-        up = w.at[level, pl.ds(0, 4), src, :, ycols(yl)]
         copy(up, up, l_s.at[level, 0], l_r.at[level, s, 0], {"batch_0": yr}).start()
+        copy(left, left, dy_s.at[level], dy_r.at[level], {"field": 1 - c}).start()
         arrived(right, y_r.at[level, s, 1])
-        down = w.at[level, pl.ds(4, 3), src, :, ycols(yr)]
         copy(down, down, l_s.at[level, 1], l_r.at[level, s, 1], {"batch_0": yl}).start()
+        copy(right, right, dy_s.at[level], dy_r.at[level], {"field": 1 - c}).start()
 
     def to_core(level, s):
         src = (z + NZ - slot_shift(s)) % NZ
         far = (y + 2) % NX
+        piece = w.at[level, :, src, :, ycols(far)]
         arrived(w.at[level, pl.ds(0, 4), src, :, ycols(far)], l_r.at[level, s, 0])
         arrived(w.at[level, pl.ds(4, 3), src, :, ycols(far)], l_r.at[level, s, 1])
-        piece = w.at[level, :, src]
-        copy(piece, piece, d_s.at[level], d_r.at[level], {"field": 1 - c}).start()
+        copy(piece, piece, dy_s.at[level], dy_r.at[level], {"field": 1 - c}).start()
 
     def tower_step(s):
         src = (z + NZ - slot_shift(s)) % NZ
@@ -267,44 +331,90 @@
 
     @pl.when(c == wide)
     def _():
-        w[:, :, z, :, ycols(y)] = w_own[:, :, :, 0:KA]
-        w[:, :, z, :, NX * NY * 128 :] = w_own[:, :, :, KA:]
-
-        @pl.loop(0, NZ + 2)
+        from_a(0, 0)
+        copy(
+            feat.at[:, :, lanes(z)],
+            a1.at[pl.ds(HALF * c, HALF), z, :, lanes(p)],
+            a2a_s.at[1], a2a_r.at[0], {"field": tall},
+        ).start()
+        examples_out()
+
+        @pl.loop(1, NZ + 3)
         def _(i):
             @pl.when(i < NZ)
             def _():
-                from_z(0, i)
-
-            @pl.when((i > 0) & (i < NZ + 1))
-            def _():
-                from_y(0, i - 1)
-
-            @pl.when(i > 1)
-            def _():
-                to_core(0, i - 2)
-
-            @pl.when(i < NZ)
-            def _():
-                relay_step(i)
-
-        from_z(1, 0)
+                from_a(0, i)
+
+            @pl.when(i > 2)
+            def _():
+                from_b(0, i - 3)
+
+            @pl.when(i == NZ)
+            def _():
+                from_a(1, 0)
+
+            @pl.when((i > 1) & (i < NZ + 2))
+            def _():
+                relay_step(i - 2)
+
+        from_a(1, 1)
+        from_a(1, 2)
+        from_b(1, 0)
+        tower_step(0)
 
         @pl.loop(0, NZ)
         def _(i):
             far_step(i)
 
+        arrived(w.at[0, :, :, :, pl.ds(0, 3 * KA)], dy_r.at[0])
+
     @pl.when(c == tall)
     def _():
-        @pl.loop(0, NZ)
+        examples_out()
+        for step in range(1, NX):
+            to = (x + step) % NX
+            copy(
+                c_own, cands.at[NX * y + x], c_s.at[0], c_r.at[0], {"batch_1": to, "field": 1 - to // 2}
+            ).start()
+        to_y(0, 0)
+        example_step(0)
+
+        @pl.loop(1, NZ + 3)
         def _(i):
-            example_step(i)
-            relay_step(i)
+            @pl.when((i > 1) & (i < NZ))
+            def _():
+                to_y(0, i)
+
+            @pl.when(i < NZ + 1)
+            def _():
+                from_y(0, i - 1)
+
+            @pl.when(i == 1)
+            def _():
+                to_y(0, i)
+
+            @pl.when(i < NZ)
+            def _():
+                example_step(i)
+
+            @pl.when(i == NZ)
+            def _():
+                to_y(1, 0)
+
+            @pl.when(i == NZ + 1)
+            def _():
+                to_y(1, 1)
+
+            @pl.when((i > 1) & (i < NZ + 2))
+            def _():
+                relay_step(i - 2)
+
+            @pl.when(i > 2)
+            def _():
+                to_core(0, i - 3)
 
         tower_step(0)
-        arrived(w.at[0], d_r.at[0])
-
-    base = HALF * wide + 6 * p
+        arrived(w.at[0, :, :, :, rest], db_r.at[0])
 
     @pl.loop(0, BLK)
     def _(f):
@@ -319,59 +429,63 @@
 
     @pl.when(c == wide)
     def _():
-        tower_step(0)
-
-        @pl.loop(1, NZ + 2)
+        @pl.loop(3, NZ + 3)
         def _(i):
             @pl.when(i < NZ)
             def _():
-                from_z(1, i)
-
-            from_y_ok = i < NZ + 1
-
-            @pl.when(from_y_ok)
+                from_a(1, i)
+
+            @pl.when(i > 3)
+            def _():
+                from_b(1, i - 3)
+                tower_step(i - 3)
+
+            @pl.when(i == 4)
+            def _():
+                second_step(0)
+
+            @pl.when(i == 6)
+            def _():
+                second_step(1)
+
+        second_far()
+        arrived(w.at[1, :, :, :, pl.ds(0, 3 * KA)], dy_r.at[1])
+
+    @pl.when(c == tall)
+    def _():
+        got = cands.at[pl.ds(NX * y, NX)]
+
+        @pl.loop(1, NZ + 3)
+        def _(i):
+            @pl.when((i > 1) & (i < NZ))
+            def _():
+                to_y(1, i)
+
+            @pl.when(i < NZ + 1)
             def _():
                 from_y(1, i - 1)
 
-            @pl.when(i > 1)
-            def _():
-                to_core(1, i - 2)
-
-            @pl.when(i < NZ)
-            def _():
-                tower_step(i)
+            @pl.when(i > 2)
+            def _():
+                to_core(1, i - 3)
+
+            @pl.when(i > 3)
+            def _():
+                tower_step(i - 3)
 
             @pl.when(i == 3)
             def _():
                 second_step(0)
 
-            @pl.when(i == 6)
+            @pl.when(i == 5)
             def _():
                 second_step(1)
 
-        second_far()
-
-    @pl.when(c == tall)
-    def _():
-        got = cands.at[pl.ds(NX * y, NX)]
         arrived(cands.at[pl.ds(NX * y, NX - 1)], c_r.at[0])
         for step in range(1, NX):
             copy(got, got, c_s.at[1], c_r.at[1], {"batch_0": (y + step) % NX}).start()
-
-        @pl.loop(1, NZ)
-        def _(i):
-            tower_step(i)
-
-            @pl.when(i == 3)
-            def _():
-                second_step(0)
-
-            @pl.when(i == 5)
-            def _():
-                second_step(1)
-
         second_far()
-        arrived(w.at[1], d_r.at[1])
+        arrived(w.at[1, :, :, :, rest], db_r.at[1])
 
     @pl.loop(0, BLK)
     def _(f):
@@ -384,24 +498,61 @@
 
     arrived(t.at[:, c], td_r)
 
-    @pl.loop(0, NZ)
-    def _(k):
+    def tower(k):
         lhs = t[k, :, :, 0 : BLK * 128].reshape(128, BLK * 128)
         prod = jnp.dot(lhs, cur2[...].reshape(BLK * 128, 256), preferred_element_type=F32)
         part[pl.ds(128 * k, 128)] = prod.astype(BF16)
         mine[pl.ds(128 * k, 128)] = prod
 
+    def far_sum(h):
+        for j in range(2):
+            @pl.when((x + NX - first - j) % NX == 2)
+            def _():
+                to = (xr, xl)[h]
+                copy(
+                    part.at[pl.ds(512 * h, 512), pl.ds(128 * j, 128)], hop, rs_s.at[h], hop_r, {"batch_1": to}
+                ).start()
+
+    for h in range(2):
+        @pl.loop(4 * h, 4 * h + 4)
+        def _(k):
+            tower(k)
+
+        far_sum(h)
+
+    for r, own, added, way in ((1, 0, 512, xl), (3, 512, 0, xr)):
+        for j in range(2):
+            @pl.when((x + NX - first - j) % NX == r)
+            def _():
+                cols = pl.ds(128 * j, 128)
+                slot = rs.at[r // 2]
+                copy(
+                    part.at[pl.ds(own, 512), cols], slot.at[pl.ds(own, 512)], rs_s.at[2], rs_r, {"batch_1": way}
+                ).start()
+                arrived(hop, hop_r)
+                summed[...] = (mine[pl.ds(added, 512), cols] + hop[...].astype(F32)).astype(BF16)
+                copy(summed, slot.at[pl.ds(added, 512)], rs_s.at[3], rs_r, {"batch_1": way}).start()
+
+    @pl.when(c == tall)
+    def _():
+        arrived(rs, rs_r)
+
     for j in range(2):
-        @pl.when(x != first + j)
-        def _():
-            r = (x + NX - first - j) % NX
-            copy(
-                part.at[:, pl.ds(128 * j, 128)], rs.at[r - 1], rs_s.at[j], rs_r, {"batch_1": first + j}
-            ).start()
+        r = (x + NX - first - j) % NX
+
+        @pl.when(r == 2)
+        def _():
+            arrived(hop, rs_s.at[0])
+            arrived(hop, rs_s.at[1])
+
+        @pl.when((r == 1) | (r == 3))
+        def _():
+            arrived(hop, rs_s.at[2])
+            arrived(hop, rs_s.at[3])
 
     @pl.loop(0, 2 * NZ)
     def _(i):
-        j, to = i // NZ, i % NZ
+        j, to = i // NZ, (z + slot_shift(i % NZ)) % NZ
         where = {"batch_1": first + j, "dim": to, "field": wide}
         copy(
             cur2.at[pl.ds(p, 6), to, :, lanes(j)],
@@ -419,15 +570,15 @@
 
     @pl.when(c == tall)
     def _():
-        arrived(rs, rs_r)
         here = lanes(p)
         bias = t[:, :, :, BLK * 128 + 128 :].reshape(UNITS, 128).astype(F32)
         bias = bias[:, 0:1] + bias[:, 1:2] + bias[:, 2:3]
-        total = mine[:, here] + rs[0].astype(F32) + rs[1].astype(F32) + rs[2].astype(F32)
+        total = mine[:, here] + rs[0].astype(F32) + rs[1].astype(F32)
         hidden = jnp.maximum(total + bias, 0.0).astype(BF16)
         qw = t[:, :, :, BLK * 128 : BLK * 128 + 128].reshape(UNITS, 128)
         query = lax.dot_general(qw, hidden, (((0,), (0,)), ((), ())), preferred_element_type=F32)
-        query = (query + user_t[...].astype(F32)).astype(BF16)
+        u_copy.wait()
+        query = (query + u_own[...].astype(F32).T).astype(BF16)
 
         arrived(cands.at[pl.ds(0, 3 * NX)], c_r.at[1])
         scale = 1.0 / math.sqrt(128)
@@ -439,7 +590,7 @@
 
         top = lax.fori_loop(0, NX * NX, scores, jnp.full((8, 128), -1e30, F32))
         top = jnp.max(top, axis=0, keepdims=True)
-        wanted = target[0:1, :]
+        wanted = target[pl.ds(z, 1), :]
         index = lax.broadcasted_iota(jnp.int32, (256, 128), 0)
 
         def sums(k, carry):
@@ -474,6 +625,12 @@
         arrived(cands.at[pl.ds(0, 3 * NX)], c_s.at[1])
         for d in range(2):
             arrived(a1.at[pl.ds(0, FIELDS), :, :, pl.ds(0, 128)], ag1_s.at[d])
+        for level in range(2):
+            for d in range(2):
+                arrived(w.at[level, :, :, :, pl.ds(0, KA)], y_s.at[level, d])
+            arrived(w.at[level, pl.ds(0, 4), :, :, pl.ds(0, KA)], l_s.at[level, 0])
+            arrived(w.at[level, pl.ds(4, 3), :, :, pl.ds(0, KA)], l_s.at[level, 1])
+            arrived(w.at[level, :, :, :, pl.ds(0, 3 * KA)], dy_s.at[level])
 
     @pl.when(c == wide)
     def _():
@@ -484,11 +641,8 @@
             arrived(w.at[level, :, pl.ds(0, 3), :, pl.ds(0, KA)], z_s.at[level, 1, 0])
             arrived(w.at[level, :, pl.ds(0, 3), :, rest], z_s.at[level, 0, 1])
             arrived(w.at[level, :, pl.ds(0, 4), :, rest], z_s.at[level, 1, 1])
-            arrived(w.at[level, :, :, :, pl.ds(0, KA)], y_s.at[level, 0])
-            arrived(w.at[level, :, :, :, pl.ds(0, KA)], y_s.at[level, 1])
-            arrived(w.at[level, pl.ds(0, 4), :, :, pl.ds(0, KA)], l_s.at[level, 0])
-            arrived(w.at[level, pl.ds(4, 3), :, :, pl.ds(0, KA)], l_s.at[level, 1])
-            arrived(w.at[level], d_s.at[level])
+            arrived(w.at[level, :, :, :, pl.ds(0, KA)], da_s.at[level])
+            arrived(w.at[level, :, :, :, rest], db_s.at[level])
 
     arrived(feat.at[:, :, pl.ds(0, 128 * (NZ - 1))], a2a_s.at[0])
     for j in range(2):
@@ -501,10 +655,6 @@
         @pl.when(r == 3)
         def _():
             arrived(a1.at[pl.ds(0, HALF), :, :, pl.ds(0, 128)], ag1_ls.at[1])
-
-        @pl.when(r != 0)
-        def _():
-            arrived(rs.at[0], rs_s.at[j])
 
     for h in range(2):
         for d in range(2):
@@ -516,49 +666,22 @@
     arrived(t.at[:, 0], td_s)
     arrived(cur2.at[pl.ds(0, 6)], o_s.at[0])
     arrived(cur2.at[0, pl.ds(0, 4)], o_s.at[1])
+    for k in range(NZ):
+        loss_out[k : k + 1] = loss[k, 0:1]
     arrived(out, o_r)
 
 
-def three_parts(v):
-    hi = lax.reduce_precision(v, 8, 7)
-    mid = lax.reduce_precision(v - hi, 8, 7)
-    low = (v - hi) - mid
-    return jnp.stack([hi, mid, low], axis=-1).astype(BF16)
-
-
-def lane_block(parts):
-    return jnp.pad(parts, [(0, 0)] * (parts.ndim - 1) + [(0, 128 - parts.shape[-1])])
-
-
 def body(features, cross_weight, cross_bias, tower_weight, tower_bias, query_weight, user_vec, candidates, positive):
-    x = lax.axis_index("batch_1")
-    y = lax.axis_index("batch_0")
-    z = lax.axis_index("dim")
-    p = x % 2
-
-    rows = lax.dynamic_slice_in_dim(cross_weight, 6 * p, BLK, 1)
-    own = lax.dynamic_slice_in_dim(rows, NY * y, NY, 3)
-    rest = rows[:, :, :, NX * NY :]
-    bias = lane_block(three_parts(lax.dynamic_slice_in_dim(cross_bias, 6 * p, BLK, 1)))
-    w_own = jnp.concatenate([own, rest, bias[:, :, :, None]], axis=3).reshape(2, BLK, SUB, KA + KR)
-
-    cols = lax.dynamic_slice_in_dim(tower_weight, (13 * x) // 2, BLK, 1).reshape(64, BLK * 128)
-    at = lax.broadcasted_iota(jnp.int32, (1, BLK * 128), 1) - 64 * p
-    cols = jnp.where((at >= 0) & (at < 832), cols, jnp.zeros_like(cols))
-    t_own = jnp.concatenate([cols, query_weight, lane_block(three_parts(tower_bias))], axis=1)
-
-    user_t = lax.dynamic_slice_in_dim(user_vec, 128 * z, 128, 0).T
-    target = jnp.broadcast_to(lax.dynamic_slice_in_dim(positive, 128 * z, 128, 0)[None], (8, 128))
-
     vmem = pl.BlockSpec(memory_space=pltpu.VMEM)
+    hbm = pl.BlockSpec(memory_space=pl.ANY)
     dma = pltpu.SemaphoreType.DMA
     out, loss = pl.pallas_call(
         kernel,
         out_shape=(
             jax.ShapeDtypeStruct((HALF, SUB, 1024), BF16),
-            jax.ShapeDtypeStruct((NZ, 8, 128), F32),
+            jax.ShapeDtypeStruct((NZ, 128), F32),
         ),
-        in_specs=[vmem] * 6,
+        in_specs=[vmem, hbm, vmem, hbm, vmem, vmem, vmem, hbm, vmem],
         out_specs=(vmem, vmem),
         scratch_shapes=[
             pltpu.VMEM((KB, NZ, SUB, 256), BF16),
@@ -569,26 +692,41 @@
             pltpu.VMEM((BLK, NZ, SUB, 256), BF16),
             pltpu.VMEM((UNITS, 256), BF16),
             pltpu.VMEM((UNITS, 256), F32),
-            pltpu.VMEM((3, UNITS, 128), BF16),
+            pltpu.VMEM((2, UNITS, 128), BF16),
+            pltpu.VMEM((UNITS // 2, 128), BF16),
+            pltpu.VMEM((UNITS // 2, 128), BF16),
             pltpu.VMEM((NX * NX, 256, 128), BF16),
             pltpu.VMEM((NX * NX, 256, 128), F32),
+            pltpu.VMEM((128, 128), BF16),
+            pltpu.VMEM((NZ, 8, 128), F32),
+            dma((2, NY + NREST - 1)), dma((BLK,)), dma,
             dma((2,)), dma((NZ,)),
             dma((2,)), dma((2, NZ, 2)), dma((2,)),
             dma((2, 2)), dma((2, 2)), dma((2,)), dma((2,)),
             dma((2, 2, 2)), dma((2, NZ, 2)),
             dma((2, 2)), dma((2, NZ, 2)),
             dma((2, 2)), dma((2, NZ, 2)),
-            dma((2,)), dma((2,)),
+            dma((2,)), dma((2, NZ)), dma((2,)), dma((2,)), dma((2,)), dma((2,)),
             dma((4,)), dma((9,)), dma, dma,
             dma((2,)), dma((2,)),
-            dma((2,)), dma,
+            dma((4,)), dma, dma,
             dma((2,)), dma,
             dma((3,)), dma,
         ],
-        compiler_params=pltpu.CompilerParams(has_side_effects=True, vmem_limit_bytes=60 * 1024 * 1024),
+        compiler_params=pltpu.CompilerParams(collective_id=0, has_side_effects=True, vmem_limit_bytes=60 * 1024 * 1024),
         name="dcn",
-    )(features, w_own, t_own, candidates, user_t, target)
-    return out, loss[:, 0, :].reshape(1024)
+    )(
+        features,
+        cross_weight.transpose(0, 1, 3, 2, 4),
+        cross_bias.transpose(1, 0, 2),
+        tower_weight.transpose(1, 0, 2),
+        tower_bias.reshape(1, 64),
+        query_weight,
+        candidates,
+        user_vec,
+        positive.reshape(NZ, 128),
+    )
+    return out, loss.reshape(1024)
 
 
 def solution(mesh):

time: 136 us -> 109 us (0.80)
  Pallas kernels: 125 us -> 104 us
  local copies, waits for them, and re-layouts: 6.76 us -> 3.07 us
  other arithmetic: 3.55 us -> 0 us
    pallas_call x1, Pallas kernels: 125 us -> 104 us  [body(): pl.pallas_call(kernel, out_shape=(jax.ShapeDtypeStruct((HALF, SUB, 1024),...]
    dynamic_slice x3 -> x0, local copies, waits for them, and re-layouts: 1.54 us -> none  [the longest x1 0.76 us: body(): user_t = lax.dynamic_slice_in_dim(user_vec, 128 * z, 128, 0).T]
    slice x2 -> x0, local copies, waits for them, and re-layouts: 1.37 us -> none  [the longest x1 1.35 us: body(): return (out, loss[:, 0, :].reshape(1024))]
    unnamed x8 -> x2, local copies, waits for them, and re-layouts: 2.6 us -> 3.07 us
where the time goes in v2:
time: 109 us; the launch traced here: 108 us
  Pallas kernels  104 us (95%)
  local copies, waits for them, and re-layouts  3.07 us (3%)
    pallas_call x1, Pallas kernels, body(): pl.pallas_call(kernel, out_shape=(jax.ShapeDtypeStruct((HALF, SUB, 1024),...  104 us
    unnamed x2, local copies, waits for them, and re-layouts  3.07 us

profile of v2, /device:TPU:7, one launch (start us, length us, event | category | flops | bytes accessed | tf_op | source)
XLA Modules:
  0.0 107.8 jit_solution(15940724642866524075)
XLA Ops:
  0.6 104.1 %dcn.1 = (bf16[13,16,1024]{2,1,0:T(8,128)(2,1)}, f32[8,128]{1,0:T(8,128)}) custom-call(bf16[13,16,1024]{2,1,0:T(8,128)(2,1)} %feat.1, bf16[2,13,26,16,128]{4,3,2,1,0:T(8,128)(2,1)} %bitcast.6, f32[13,2,16]{2,1,0:T(2,128)} %bitcast.8, bf16[26,64,128]{2,1,0:T(8,128)(2,1)} %bitcast.7, f32[1,64]{1,0:T(1,128)} %bitcast.11, bf16[64,128]{1,0:T(8,128)(2,1)} %q_w.1, ...), custom_call_target="tpu_custom_call" | custom-call | tf_op jit(solution)/shard_map/dcn/pallas_call | solution.py:678
  104.8 1.8 %copy.13 = bf16[13,16,1024]{2,1,0:T(8,128)(2,1)} copy(bf16[13,16,1024]{2,1,0:T(8,128)(2,1)} %get-tuple-element.8) | data formatting | bytes 851968
  106.6 1.3 %copy.14 = f32[1024]{0:T(1024)} copy(f32[1024]{0:T(1024)} %bitcast.10) | data formatting | bytes 8192

commit v3 on v2

--- a/solution.py
+++ b/solution.py
@@ -120,7 +120,7 @@
     )
     ones = jnp.where(row < 3, 1.0, 0.0).astype(BF16)
     a1[FIELDS] = ones
-    a2[FIELDS * NZ : KB * NZ] = ones
+    a2[FIELDS] = ones
 
     def bias_block(values):
         n = values.shape[1]
@@ -160,8 +160,8 @@
 
     pl.semaphore_wait(barrier, 3 * NX - 3 + 2 * NZ - 2 + 1)
 
-    def examples_out():
-        @pl.loop(1, NZ)
+    def examples_out(low, high):
+        @pl.loop(low, high)
         def _(s):
             to = (z + slot_shift(s)) % NZ
             copy(
@@ -175,6 +175,10 @@
         nxt = jnp.where(s == 0, 1 + d, jnp.minimum(s + 2, NZ - 1))
         copy(ref, ref, z_s.at[level, d, k], z_r.at[level, nxt, k], {"dim": to}).start()
 
+    def hand_over(level, s):
+        ref = w.at[level, :, (z + NZ - slot_shift(s)) % NZ, :, ycols(y)]
+        copy(ref, ref, da_s.at[level], da_r.at[level, s], {"field": 1 - c}).start()
+
     def from_z(level, s, k):
         src = (z + NZ - slot_shift(s)) % NZ
         ref = w.at[level, :, src, :, rest] if k else w.at[level, :, src, :, ycols(y)]
@@ -194,9 +198,13 @@
             along_z(ref, level, s, k, 1)
 
         if k:
-            copy(ref, ref, db_s.at[level], db_r.at[level], {"field": 1 - c}).start()
+            copy(ref, ref, db_s.at[level], db_r.at[level, s], {"field": 1 - c}).start()
+        elif level == 0:
+            hand_over(level, s)
         else:
-            copy(ref, ref, da_s.at[level], da_r.at[level, s], {"field": 1 - c}).start()
+            @pl.when(s > 0)
+            def _():
+                hand_over(level, s)
 
     def from_a(level, s):
         from_z(level, s, 0)
@@ -219,10 +227,10 @@
         down = w.at[level, pl.ds(4, 3), src, :, ycols(yr)]
         arrived(left, y_r.at[level, s, 0])
         copy(up, up, l_s.at[level, 0], l_r.at[level, s, 0], {"batch_0": yr}).start()
-        copy(left, left, dy_s.at[level], dy_r.at[level], {"field": 1 - c}).start()
+        copy(left, left, dy_s.at[level], dy_r.at[level, s], {"field": 1 - c}).start()
         arrived(right, y_r.at[level, s, 1])
         copy(down, down, l_s.at[level, 1], l_r.at[level, s, 1], {"batch_0": yl}).start()
-        copy(right, right, dy_s.at[level], dy_r.at[level], {"field": 1 - c}).start()
+        copy(right, right, dy_s.at[level], dy_r.at[level, s], {"field": 1 - c}).start()
 
     def to_core(level, s):
         src = (z + NZ - slot_shift(s)) % NZ
@@ -230,7 +238,7 @@
         piece = w.at[level, :, src, :, ycols(far)]
         arrived(w.at[level, pl.ds(0, 4), src, :, ycols(far)], l_r.at[level, s, 0])
         arrived(w.at[level, pl.ds(4, 3), src, :, ycols(far)], l_r.at[level, s, 1])
-        copy(piece, piece, dy_s.at[level], dy_r.at[level], {"field": 1 - c}).start()
+        copy(piece, piece, dy_s.at[level], dy_r.at[level, s], {"field": 1 - c}).start()
 
     def tower_step(s):
         src = (z + NZ - slot_shift(s)) % NZ
@@ -308,26 +316,93 @@
                 arrived(a1.at[pl.ds(0, HALF), src, :, pl.ds(128 * j, 128)], ag1_r.at[j, s, 0])
                 arrived(a1.at[pl.ds(HALF, HALF), src, :, pl.ds(128 * j, 128)], ag1_r.at[j, s, 1])
 
-    def tiles(who, h):
-        return a2.at[pl.ds(QUART * who + 26 * h, 26)]
-
-    def second_send():
-        for h in range(2):
-            mineh = cur1.at[pl.ds(4 * p + 26 * h, 26)]
-            copy(mineh, tiles(x, h), ag2_s.at[h, 0], ag2_r.at[h, 0], {"batch_1": xr}).start()
-            copy(mineh, tiles(x, h), ag2_s.at[h, 1], ag2_r.at[h, 1], {"batch_1": xl}).start()
-
-    def second_step(h):
-        for d in ((0, 1) if h == 0 else (1, 0)):
-            who, to = ((xl, xr), (xr, xl))[d]
-            arrived(tiles(who, h), ag2_r.at[h, d])
-            if d == h:
-                copy(tiles(who, h), tiles(who, h), ag2_ls.at[h], ag2_lr.at[h], {"batch_1": to}).start()
-
-    def second_far():
-        far = (x + 2) % NX
-        arrived(tiles(far, 0), ag2_lr.at[0])
-        arrived(tiles(far, 1), ag2_lr.at[1])
+    def owned(ref, field, s, extra):
+        src = (z + NZ - slot_shift(s)) % NZ
+        return ref.at[pl.ds(field, 1 if extra else 6), src]
+
+    def with_extra(who, s, act):
+        act(13 * (who // 2) + 7 * (who % 2), False)
+
+        @pl.when(((z + NZ - slot_shift(s)) % NZ) // 4 == who % 2)
+        def _():
+            act(13 * (who // 2) + 6, True)
+
+    def second_send(s):
+        def act(field, extra):
+            kind = 1 if extra else 0
+            mineh = owned(cur1, field - base, s, extra)
+            there = owned(a2, field, s, extra)
+            copy(mineh, there, ag2_s.at[kind, 0], ag2_r.at[kind, s, 0], {"batch_1": xr}).start()
+            copy(mineh, there, ag2_s.at[kind, 1], ag2_r.at[kind, s, 1], {"batch_1": xl}).start()
+            there[...] = mineh[...]
+
+        with_extra(x, s, act)
+
+    def second_step(s):
+        for d, who, to in ((0, xl, xr), (1, xr, xl)):
+            def act(field, extra):
+                kind = 1 if extra else 0
+                piece = owned(a2, field, s, extra)
+                arrived(piece, ag2_r.at[kind, s, d])
+
+                @pl.when((z + NZ - slot_shift(s)) % 2 == 1 - d)
+                def _():
+                    copy(piece, piece, ag2_ls.at[kind, d], ag2_lr.at[kind, s], {"batch_1": to}).start()
+
+            with_extra(who, s, act)
+
+    def second_far(s):
+        def act(field, extra):
+            arrived(owned(a2, field, s, extra), ag2_lr.at[1 if extra else 0, s])
+
+        with_extra((x + 2) % NX, s, act)
+
+    def crossed(to):
+        for j in range(2):
+            where = {"batch_1": first + j, "dim": to, "field": wide}
+            copy(
+                cur2.at[pl.ds(p, 6), to, :, lanes(j)],
+                out.at[pl.ds(7 * p, 6), :, lanes(z)],
+                o_s.at[0], o_r, where,
+            ).start()
+
+            @pl.when((to // 4) == p)
+            def _():
+                copy(
+                    cur2.at[pl.ds(6 - 6 * p, 1), to, :, lanes(j)],
+                    out.at[pl.ds(6, 1), :, lanes(z)],
+                    o_s.at[1], o_r, where,
+                ).start()
+
+    def layer(level, s):
+        src = (z + NZ - slot_shift(s)) % NZ
+        lhs = w[level, :, src].reshape(BLK * SUB, KW)
+        anchor = a1[pl.ds(base, BLK), src].reshape(BLK * SUB, 256).astype(F32)
+        if level == 0:
+            rhs = a1[...].reshape(KW, 256)
+            before = anchor
+        else:
+            rhs = a2[...].reshape(KW, 256)
+            before = cur1[:, src].reshape(BLK * SUB, 256).astype(F32)
+        prod = jnp.dot(lhs, rhs, preferred_element_type=F32)
+        nxt = (anchor * prod + before).astype(BF16).reshape(BLK, SUB, 256)
+        if level == 0:
+            cur1[:, src] = nxt
+            second_send(s)
+        else:
+            cur2[:, src] = nxt
+            crossed(src)
+
+    def rows_here(level, s):
+        src = (z + NZ - slot_shift(s)) % NZ
+
+        @pl.when(c == wide)
+        def _():
+            arrived(w.at[level, :, src, :, pl.ds(0, 3 * KA)], dy_r.at[level, s])
+
+        @pl.when(c == tall)
+        def _():
+            arrived(w.at[level, :, src, :, rest], db_r.at[level, s])
 
     @pl.when(c == wide)
     def _():
@@ -337,164 +412,186 @@
             a1.at[pl.ds(HALF * c, HALF), z, :, lanes(p)],
             a2a_s.at[1], a2a_r.at[0], {"field": tall},
         ).start()
-        examples_out()
-
-        @pl.loop(1, NZ + 3)
+        hand_over(1, 0)
+        examples_out(1, 3)
+
+        @pl.loop(1, 14)
         def _(i):
             @pl.when(i < NZ)
             def _():
                 from_a(0, i)
 
-            @pl.when(i > 2)
-            def _():
-                from_b(0, i - 3)
-
-            @pl.when(i == NZ)
-            def _():
-                from_a(1, 0)
-
-            @pl.when((i > 1) & (i < NZ + 2))
-            def _():
-                relay_step(i - 2)
-
-        from_a(1, 1)
-        from_a(1, 2)
-        from_b(1, 0)
-        tower_step(0)
+            for due, low, high in ((2, 3, 5), (4, 5, 7), (5, 7, 8)):
+                @pl.when(i == due)
+                def _():
+                    examples_out(low, high)
+
+            @pl.when((i >= 4) & (i < 12))
+            def _():
+                from_b(0, i - 4)
+
+            @pl.when(i >= 6)
+            def _():
+                from_a(1, i - 6)
+
+            @pl.when((i >= 5) & (i < 13))
+            def _():
+                relay_step(i - 5)
+
+            @pl.when(i == 10)
+            def _():
+                tower_step(0)
+
+            @pl.when(i >= 11)
+            def _():
+                from_b(1, i - 11)
+
+        tower_step(1)
+        tower_step(2)
 
         @pl.loop(0, NZ)
         def _(i):
             far_step(i)
 
-        arrived(w.at[0, :, :, :, pl.ds(0, 3 * KA)], dy_r.at[0])
+        @pl.loop(0, NZ)
+        def _(s):
+            rows_here(0, s)
+            layer(0, s)
 
     @pl.when(c == tall)
     def _():
-        examples_out()
+        examples_out(1, 3)
+        to_y(0, 0)
+        to_y(1, 0)
         for step in range(1, NX):
             to = (x + step) % NX
             copy(
                 c_own, cands.at[NX * y + x], c_s.at[0], c_r.at[0], {"batch_1": to, "field": 1 - to // 2}
             ).start()
-        to_y(0, 0)
         example_step(0)
-
-        @pl.loop(1, NZ + 3)
-        def _(i):
-            @pl.when((i > 1) & (i < NZ))
-            def _():
-                to_y(0, i)
-
-            @pl.when(i < NZ + 1)
-            def _():
-                from_y(0, i - 1)
-
-            @pl.when(i == 1)
-            def _():
-                to_y(0, i)
-
-            @pl.when(i < NZ)
-            def _():
-                example_step(i)
-
-            @pl.when(i == NZ)
-            def _():
-                to_y(1, 0)
-
-            @pl.when(i == NZ + 1)
-            def _():
-                to_y(1, 1)
-
-            @pl.when((i > 1) & (i < NZ + 2))
-            def _():
-                relay_step(i - 2)
-
-            @pl.when(i > 2)
-            def _():
-                to_core(0, i - 3)
-
-        tower_step(0)
-        arrived(w.at[0, :, :, :, rest], db_r.at[0])
-
-    @pl.loop(0, BLK)
-    def _(f):
-        lhs = w[0, f].reshape(128, KW)
-        prod = jnp.dot(lhs, a1[...].reshape(KW, 256), preferred_element_type=F32)
-        anchor = a1[base + f].reshape(128, 256).astype(F32)
-        nxt = (anchor * prod + anchor).astype(BF16)
-        cur1[pl.ds(NZ * f, NZ)] = nxt.reshape(NZ, SUB, 256)
-
-    second_send()
-    a2[pl.ds(QUART * x, QUART)] = cur1[pl.ds(4 * p, QUART)]
-
-    @pl.when(c == wide)
-    def _():
-        @pl.loop(3, NZ + 3)
+        from_y(0, 0)
+
+        @pl.loop(1, 12)
         def _(i):
             @pl.when(i < NZ)
             def _():
-                from_a(1, i)
-
-            @pl.when(i > 3)
-            def _():
-                from_b(1, i - 3)
+                to_y(0, i)
+
+            for due in (1, 2, 3):
+                @pl.when(i == due)
+                def _():
+                    examples_out(2 * due + 1, min(2 * due + 3, NZ))
+
+            @pl.when(i == 1)
+            def _():
+                from_y(1, 0)
+
+            @pl.when((i > 1) & (i < NZ + 1))
+            def _():
+                from_y(0, i - 1)
+
+            @pl.when((i > 1) & (i < NZ + 1))
+            def _():
+                example_step(i - 1)
+
+            @pl.when(i >= 8)
+            def _():
+                to_y(1, i - 7)
+
+            @pl.when(i >= 10)
+            def _():
+                from_y(1, i - 9)
+
+            @pl.when(i == 11)
+            def _():
+                @pl.loop(5, NZ)
+                def _(s):
+                    to_y(1, s)
+
+            @pl.when((i >= 3) & (i < 11))
+            def _():
+                to_core(0, i - 3)
+
+            @pl.when((i >= 3) & (i < 11))
+            def _():
+                relay_step(i - 3)
+
+            @pl.when(i == 4)
+            def _():
+                to_core(1, 0)
+
+            @pl.when(i == 8)
+            def _():
+                tower_step(0)
+
+            @pl.when(i == 11)
+            def _():
+                tower_step(1)
+                tower_step(2)
+
+            @pl.when(i >= 10)
+            def _():
+                @pl.loop(0, 3)
+                def _(k):
+                    s = 3 * (i - 10) + k
+                    rows_here(0, s)
+                    layer(0, s)
+
+        @pl.loop(6, NZ)
+        def _(s):
+            rows_here(0, s)
+            layer(0, s)
+
+    @pl.when(c == wide)
+    def _():
+        @pl.loop(0, NZ)
+        def _(i):
+            @pl.when((i % 4 == 0) | (i % 4 == 1))
+            def _():
+                k = 3 + 2 * (i // 4) + i % 4
+                from_b(1, k)
+                tower_step(k)
+
+            second_step(i)
+
+        from_b(1, 7)
+        tower_step(7)
+
+    @pl.when(c == tall)
+    def _():
+        @pl.loop(5, 10)
+        def _(i):
+            from_y(1, i - 2)
+            to_core(1, i - 4)
+
+            @pl.when(i < 9)
+            def _():
+                second_step(2 * i - 10)
+                second_step(2 * i - 9)
+
+            @pl.when(i >= 6)
+            def _():
                 tower_step(i - 3)
 
-            @pl.when(i == 4)
-            def _():
-                second_step(0)
-
-            @pl.when(i == 6)
-            def _():
-                second_step(1)
-
-        second_far()
-        arrived(w.at[1, :, :, :, pl.ds(0, 3 * KA)], dy_r.at[1])
-
-    @pl.when(c == tall)
-    def _():
-        got = cands.at[pl.ds(NX * y, NX)]
-
-        @pl.loop(1, NZ + 3)
-        def _(i):
-            @pl.when((i > 1) & (i < NZ))
-            def _():
-                to_y(1, i)
-
-            @pl.when(i < NZ + 1)
-            def _():
-                from_y(1, i - 1)
-
-            @pl.when(i > 2)
-            def _():
-                to_core(1, i - 3)
-
-            @pl.when(i > 3)
-            def _():
-                tower_step(i - 3)
-
-            @pl.when(i == 3)
-            def _():
-                second_step(0)
-
-            @pl.when(i == 5)
-            def _():
-                second_step(1)
-
-        arrived(cands.at[pl.ds(NX * y, NX - 1)], c_r.at[0])
-        for step in range(1, NX):
-            copy(got, got, c_s.at[1], c_r.at[1], {"batch_0": (y + step) % NX}).start()
-        second_far()
-        arrived(w.at[1, :, :, :, rest], db_r.at[1])
-
-    @pl.loop(0, BLK)
-    def _(f):
-        lhs = w[1, f].reshape(128, KW)
-        prod = jnp.dot(lhs, a2[...].reshape(KW, 256), preferred_element_type=F32)
-        anchor = a1[base + f].reshape(128, 256).astype(F32)
-        before = cur1[pl.ds(NZ * f, NZ)].reshape(128, 256).astype(F32)
-        nxt = (anchor * prod + before).astype(BF16)
-        cur2[f] = nxt.reshape(NZ, SUB, 256)
+        to_core(1, 6)
+        tower_step(7)
+
+    @pl.loop(0, NZ)
+    def _(s):
+        second_far(s)
+
+    @pl.loop(0, NZ)
+    def _(s):
+        @pl.when((c == tall) & (s == 4))
+        def _():
+            to_core(1, 7)
+            got = cands.at[pl.ds(NX * y, NX)]
+            arrived(cands.at[pl.ds(NX * y, NX - 1)], c_r.at[0])
+            for step in range(1, NX):
+                copy(got, got, c_s.at[1], c_r.at[1], {"batch_0": (y + step) % NX}).start()
+
+        rows_here(1, s)
+        layer(1, s)
 
     arrived(t.at[:, c], td_r)
 
@@ -549,24 +646,6 @@
         def _():
             arrived(hop, rs_s.at[2])
             arrived(hop, rs_s.at[3])
-
-    @pl.loop(0, 2 * NZ)
-    def _(i):
-        j, to = i // NZ, (z + slot_shift(i % NZ)) % NZ
-        where = {"batch_1": first + j, "dim": to, "field": wide}
-        copy(
-            cur2.at[pl.ds(p, 6), to, :, lanes(j)],
-            out.at[pl.ds(7 * p, 6), :, lanes(z)],
-            o_s.at[0], o_r, where,
-        ).start()
-
-        @pl.when((to // 4) == p)
-        def _():
-            copy(
-                cur2.at[pl.ds(6 - 6 * p, 1), to, :, lanes(j)],
-                out.at[pl.ds(6, 1), :, lanes(z)],
-                o_s.at[1], o_r, where,
-            ).start()
 
     @pl.when(c == tall)
     def _():
@@ -588,7 +667,7 @@
             logits[k] = got
             return jnp.maximum(top, jnp.max(got.reshape(32, 8, 128), axis=0))
 
-        top = lax.fori_loop(0, NX * NX, scores, jnp.full((8, 128), -1e30, F32))
+        top = lax.fori_loop(0, NX * NX, scores, jnp.full((8, 128), -1e30, F32), unroll=4)
         top = jnp.max(top, axis=0, keepdims=True)
         wanted = target[pl.ds(z, 1), :]
         index = lax.broadcasted_iota(jnp.int32, (256, 128), 0)
@@ -604,7 +683,7 @@
             )
 
         zero = jnp.zeros((8, 128), F32)
-        total, picked = lax.fori_loop(0, NX * NX, sums, (zero, zero))
+        total, picked = lax.fori_loop(0, NX * NX, sums, (zero, zero), unroll=4)
         total = jnp.sum(total, axis=0, keepdims=True)
         picked = jnp.sum(picked, axis=0, keepdims=True)
         result = top + jnp.log(total) - picked
@@ -656,10 +735,11 @@
         def _():
             arrived(a1.at[pl.ds(0, HALF), :, :, pl.ds(0, 128)], ag1_ls.at[1])
 
-    for h in range(2):
-        for d in range(2):
-            arrived(tiles(0, h), ag2_s.at[h, d])
-        arrived(tiles(0, h), ag2_ls.at[h])
+    for d in range(2):
+        arrived(a2.at[pl.ds(0, 6)], ag2_s.at[0, d])
+        arrived(a2.at[0, pl.ds(0, 4)], ag2_s.at[1, d])
+        arrived(a2.at[pl.ds(0, 6), pl.ds(0, 4)], ag2_ls.at[0, d])
+        arrived(a2.at[0, pl.ds(0, 2)], ag2_ls.at[1, d])
     for d in range(2):
         arrived(t.at[pl.ds(0, 3), 0], t_s.at[d])
         arrived(t.at[0, 0, pl.ds(0, 32)], t_s.at[2 + d])
@@ -678,17 +758,17 @@
     out, loss = pl.pallas_call(
         kernel,
         out_shape=(
-            jax.ShapeDtypeStruct((HALF, SUB, 1024), BF16),
-            jax.ShapeDtypeStruct((NZ, 128), F32),
+            pltpu.VMEM((HALF, SUB, 1024), BF16),
+            pltpu.VMEM((NZ, 128), F32),
         ),
         in_specs=[vmem, hbm, vmem, hbm, vmem, vmem, vmem, hbm, vmem],
         out_specs=(vmem, vmem),
         scratch_shapes=[
             pltpu.VMEM((KB, NZ, SUB, 256), BF16),
-            pltpu.VMEM((KB * NZ, SUB, 256), BF16),
+            pltpu.VMEM((KB, NZ, SUB, 256), BF16),
             pltpu.VMEM((2, BLK, NZ, SUB, KW), BF16),
             pltpu.VMEM((NZ, 2, 64, TC), BF16),
-            pltpu.VMEM((BLK * NZ, SUB, 256), BF16),
+            pltpu.VMEM((BLK, NZ, SUB, 256), BF16),
             pltpu.VMEM((BLK, NZ, SUB, 256), BF16),
             pltpu.VMEM((UNITS, 256), BF16),
             pltpu.VMEM((UNITS, 256), F32),
@@ -702,11 +782,11 @@
             dma((2, NY + NREST - 1)), dma((BLK,)), dma,
             dma((2,)), dma((NZ,)),
             dma((2,)), dma((2, NZ, 2)), dma((2,)),
-            dma((2, 2)), dma((2, 2)), dma((2,)), dma((2,)),
+            dma((2, 2)), dma((2, NZ, 2)), dma((2, 2)), dma((2, NZ)),
             dma((2, 2, 2)), dma((2, NZ, 2)),
             dma((2, 2)), dma((2, NZ, 2)),
             dma((2, 2)), dma((2, NZ, 2)),
-            dma((2,)), dma((2, NZ)), dma((2,)), dma((2,)), dma((2,)), dma((2,)),
+            dma((2,)), dma((2, NZ)), dma((2,)), dma((2, NZ)), dma((2,)), dma((2, NZ)),
             dma((4,)), dma((9,)), dma, dma,
             dma((2,)), dma((2,)),
             dma((4,)), dma, dma,

time: 109 us -> 95.5 us (0.88)
  Pallas kernels: 104 us -> 92.6 us
  local copies, waits for them, and re-layouts: 3.07 us -> 1.35 us
    pallas_call x1, Pallas kernels: 104 us -> 92.6 us  [body(): pl.pallas_call(kernel, out_shape=(pltpu.VMEM((HALF, SUB, 1024), BF16), pl...]
    unnamed x2, local copies, waits for them, and re-layouts: 3.07 us -> 1.35 us
where the time goes in v3:
time: 95.5 us; the launch traced here: 94.6 us
  Pallas kernels  92.6 us (97%)
  local copies, waits for them, and re-layouts  1.35 us (1%)
    pallas_call x1, Pallas kernels, body(): pl.pallas_call(kernel, out_shape=(pltpu.VMEM((HALF, SUB, 1024), BF16), pl...  92.6 us

profile of v3, /device:TPU:7, one launch (start us, length us, event | category | flops | bytes accessed | tf_op | source)
XLA Modules:
  0.0 94.6 jit_solution(16722415867223345004)
XLA Ops:
  0.6 92.6 %dcn.1 = (bf16[13,16,1024]{2,1,0:T(8,128)(2,1)S(1)}, f32[8,128]{1,0:T(8,128)S(1)}) custom-call(bf16[13,16,1024]{2,1,0:T(8,128)(2,1)} %feat.1, bf16[2,13,26,16,128]{4,3,2,1,0:T(8,128)(2,1)} %bitcast.7, f32[13,2,16]{2,1,0:T(2,128)} %bitcast.9, bf16[26,64,128]{2,1,0:T(8,128)(2,1)} %bitcast.8, f32[1,64]{1,0:T(1,128)} %bitcast.11, bf16[64,128]{1,0:T(8,128)(2,1)} %q_w.1, ...), custom_call_target="tpu_custom_call" | custom-call | tf_op jit(solution)/shard_map/dcn/pallas_call | solution.py:758
  93.2 0.8 copy.13
  94.0 0.6 copy.14

commit v4 on v3

--- a/solution.py
+++ b/solution.py
@@ -26,7 +26,7 @@
 KA = NY * 128
 KR = NREST * 128
 KW = KB * 128
-QUART = 52
+GROUP = 2
 TC = BLK * 128 + 256
 UNITS = 1024
 
@@ -94,7 +94,7 @@
     def own_copy(level, k):
         field = NY * y + k if k < NY else NX * NY + k - NY
         return pltpu.make_async_copy(
-            c_w.at[level, pl.ds(6 * p, BLK), field], w.at[level, :, z, :, lanes(field)], w_l.at[level, k]
+            c_w.at[level, pl.ds(6 * p, BLK), field], w.at[level, :, z, :, lanes(field)], w_l.at[level]
         )
 
     @pl.when(c == wide)
@@ -103,7 +103,7 @@
             own_copy(level, k).start()
 
     t_copies = [
-        pltpu.make_async_copy(t_w.at[base + k], t.at[z, c, :, pl.ds(128 * k, 128)], t_l.at[k])
+        pltpu.make_async_copy(t_w.at[base + k], t.at[z, c, :, pl.ds(128 * k, 128)], t_l)
         for k in range(BLK)
     ]
     for cp in t_copies:
@@ -143,16 +143,15 @@
             for level in range(2):
                 w[level, f, z, :, FIELDS * 128 :] = bias_block(c_b[6 * p + f, level : level + 1])
 
-        for level, k in own_w:
-            own_copy(level, k).wait()
+        for level in range(2):
+            arrived(w.at[level, :, z, :, pl.ds(0, 128 * (NY + NREST - 1))], w_l.at[level])
 
     @pl.when(c == tall)
     def _():
         a1[pl.ds(HALF * c, HALF), z, :, lanes(p)] = feat[:, :, lanes(z)]
         cands[NX * y + x] = c_own[...]
 
-    for cp in t_copies:
-        cp.wait()
+    arrived(t.at[z, c, :, pl.ds(0, 128 * BLK)], t_l)
     lane64 = lax.broadcasted_iota(jnp.int32, (64, 128), 1)
     edge = lanes((BLK - 1) * (1 - p))
     kept = (lane64 < 64) == (p == 0)
@@ -198,7 +197,7 @@
             along_z(ref, level, s, k, 1)
 
         if k:
-            copy(ref, ref, db_s.at[level], db_r.at[level, s], {"field": 1 - c}).start()
+            copy(ref, ref, db_s.at[level], db_r.at[level], {"field": 1 - c}).start()
         elif level == 0:
             hand_over(level, s)
         else:
@@ -226,18 +225,17 @@
         up = w.at[level, pl.ds(0, 4), src, :, ycols(yl)]
         down = w.at[level, pl.ds(4, 3), src, :, ycols(yr)]
         arrived(left, y_r.at[level, s, 0])
-        copy(up, up, l_s.at[level, 0], l_r.at[level, s, 0], {"batch_0": yr}).start()
+        copy(up, up, l_s.at[level, 0], l_r.at[level, s], {"batch_0": yr}).start()
         copy(left, left, dy_s.at[level], dy_r.at[level, s], {"field": 1 - c}).start()
         arrived(right, y_r.at[level, s, 1])
-        copy(down, down, l_s.at[level, 1], l_r.at[level, s, 1], {"batch_0": yl}).start()
+        copy(down, down, l_s.at[level, 1], l_r.at[level, s], {"batch_0": yl}).start()
         copy(right, right, dy_s.at[level], dy_r.at[level, s], {"field": 1 - c}).start()
 
     def to_core(level, s):
         src = (z + NZ - slot_shift(s)) % NZ
         far = (y + 2) % NX
         piece = w.at[level, :, src, :, ycols(far)]
-        arrived(w.at[level, pl.ds(0, 4), src, :, ycols(far)], l_r.at[level, s, 0])
-        arrived(w.at[level, pl.ds(4, 3), src, :, ycols(far)], l_r.at[level, s, 1])
+        arrived(piece, l_r.at[level, s])
         copy(piece, piece, dy_s.at[level], dy_r.at[level, s], {"field": 1 - c}).start()
 
     def tower_step(s):
@@ -285,8 +283,8 @@
         def _():
             arrived(whole, a2a_r.at[dz])
 
-        copy(whole, whole, ag1_s.at[0], ag1_r.at[p, s, 0], {"batch_1": xr}).start()
-        copy(whole, whole, ag1_s.at[1], ag1_r.at[p, s, 1], {"batch_1": xl}).start()
+        copy(whole, whole, ag1_s.at[0], ag1_r.at[p, s], {"batch_1": xr}).start()
+        copy(whole, whole, ag1_s.at[1], ag1_r.at[p, s], {"batch_1": xl}).start()
 
     def relay_step(s):
         src = (z + NZ - slot_shift(s)) % NZ
@@ -296,15 +294,15 @@
 
             @pl.when(r == 1)
             def _():
-                arrived(whole, ag1_r.at[j, s, 0])
+                arrived(whole, ag1_r.at[j, s])
                 half = a1.at[pl.ds(0, HALF), src, :, pl.ds(128 * j, 128)]
-                copy(half, half, ag1_ls.at[0], ag1_r.at[j, s, 0], {"batch_1": xr}).start()
+                copy(half, half, ag1_ls.at[0], ag1_r.at[j, s], {"batch_1": xr}).start()
 
             @pl.when(r == 3)
             def _():
-                arrived(whole, ag1_r.at[j, s, 1])
+                arrived(whole, ag1_r.at[j, s])
                 half = a1.at[pl.ds(HALF, HALF), src, :, pl.ds(128 * j, 128)]
-                copy(half, half, ag1_ls.at[1], ag1_r.at[j, s, 1], {"batch_1": xl}).start()
+                copy(half, half, ag1_ls.at[1], ag1_r.at[j, s], {"batch_1": xl}).start()
 
     def far_step(s):
         src = (z + NZ - slot_shift(s)) % NZ
@@ -313,85 +311,86 @@
 
             @pl.when(r == 2)
             def _():
-                arrived(a1.at[pl.ds(0, HALF), src, :, pl.ds(128 * j, 128)], ag1_r.at[j, s, 0])
-                arrived(a1.at[pl.ds(HALF, HALF), src, :, pl.ds(128 * j, 128)], ag1_r.at[j, s, 1])
-
-    def owned(ref, field, s, extra):
-        src = (z + NZ - slot_shift(s)) % NZ
-        return ref.at[pl.ds(field, 1 if extra else 6), src]
-
-    def with_extra(who, s, act):
-        act(13 * (who // 2) + 7 * (who % 2), False)
-
-        @pl.when(((z + NZ - slot_shift(s)) % NZ) // 4 == who % 2)
-        def _():
-            act(13 * (who // 2) + 6, True)
+                arrived(a1.at[pl.ds(0, FIELDS), src, :, pl.ds(128 * j, 128)], ag1_r.at[j, s])
+
+    def owned(who, src, act):
+        whole = src // 4 == who % 2
+
+        @pl.when(whole)
+        def _():
+            act(HALF * (who // 2) + 6 * (who % 2), 7)
+
+        @pl.when(jnp.logical_not(whole))
+        def _():
+            act(HALF * (who // 2) + 7 * (who % 2), 6)
 
     def second_send(s):
-        def act(field, extra):
-            kind = 1 if extra else 0
-            mineh = owned(cur1, field - base, s, extra)
-            there = owned(a2, field, s, extra)
-            copy(mineh, there, ag2_s.at[kind, 0], ag2_r.at[kind, s, 0], {"batch_1": xr}).start()
-            copy(mineh, there, ag2_s.at[kind, 1], ag2_r.at[kind, s, 1], {"batch_1": xl}).start()
+        src = (z + NZ - slot_shift(s)) % NZ
+
+        def act(field, n):
+            mineh = cur1.at[pl.ds(field - base, n), src]
+            there = a2.at[pl.ds(field, n), src]
+            copy(mineh, there, ag2_s.at[0], ag2_r.at[s, 0], {"batch_1": xr}).start()
+            copy(mineh, there, ag2_s.at[1], ag2_r.at[s, 1], {"batch_1": xl}).start()
             there[...] = mineh[...]
 
-        with_extra(x, s, act)
+        owned(x, src, act)
 
     def second_step(s):
+        src = (z + NZ - slot_shift(s)) % NZ
         for d, who, to in ((0, xl, xr), (1, xr, xl)):
-            def act(field, extra):
-                kind = 1 if extra else 0
-                piece = owned(a2, field, s, extra)
-                arrived(piece, ag2_r.at[kind, s, d])
-
-                @pl.when((z + NZ - slot_shift(s)) % 2 == 1 - d)
+            def act(field, n):
+                piece = a2.at[pl.ds(field, n), src]
+                arrived(piece, ag2_r.at[s, d])
+
+                @pl.when(src % 2 == 1 - d)
                 def _():
-                    copy(piece, piece, ag2_ls.at[kind, d], ag2_lr.at[kind, s], {"batch_1": to}).start()
-
-            with_extra(who, s, act)
+                    copy(piece, piece, ag2_ls.at[d], ag2_lr.at[s], {"batch_1": to}).start()
+
+            owned(who, src, act)
 
     def second_far(s):
-        def act(field, extra):
-            arrived(owned(a2, field, s, extra), ag2_lr.at[1 if extra else 0, s])
-
-        with_extra((x + 2) % NX, s, act)
+        src = (z + NZ - slot_shift(s)) % NZ
+
+        def act(field, n):
+            arrived(a2.at[pl.ds(field, n), src], ag2_lr.at[s])
+
+        owned((x + 2) % NX, src, act)
 
     def crossed(to):
-        for j in range(2):
-            where = {"batch_1": first + j, "dim": to, "field": wide}
-            copy(
-                cur2.at[pl.ds(p, 6), to, :, lanes(j)],
-                out.at[pl.ds(7 * p, 6), :, lanes(z)],
-                o_s.at[0], o_r, where,
-            ).start()
-
-            @pl.when((to // 4) == p)
-            def _():
+        def act(field, n):
+            for j in range(2):
                 copy(
-                    cur2.at[pl.ds(6 - 6 * p, 1), to, :, lanes(j)],
-                    out.at[pl.ds(6, 1), :, lanes(z)],
-                    o_s.at[1], o_r, where,
+                    cur2.at[pl.ds(field - base, n), to, :, lanes(j)],
+                    out.at[pl.ds(field - HALF * wide, n), :, lanes(z)],
+                    o_s, o_r, {"batch_1": first + j, "dim": to, "field": wide},
                 ).start()
 
-    def layer(level, s):
-        src = (z + NZ - slot_shift(s)) % NZ
-        lhs = w[level, :, src].reshape(BLK * SUB, KW)
-        anchor = a1[pl.ds(base, BLK), src].reshape(BLK * SUB, 256).astype(F32)
-        if level == 0:
-            rhs = a1[...].reshape(KW, 256)
-            before = anchor
-        else:
-            rhs = a2[...].reshape(KW, 256)
-            before = cur1[:, src].reshape(BLK * SUB, 256).astype(F32)
-        prod = jnp.dot(lhs, rhs, preferred_element_type=F32)
-        nxt = (anchor * prod + before).astype(BF16).reshape(BLK, SUB, 256)
-        if level == 0:
-            cur1[:, src] = nxt
-            second_send(s)
-        else:
-            cur2[:, src] = nxt
-            crossed(src)
+        owned(x, to, act)
+
+    def layer(level, group):
+        srcs = [(z + NZ - slot_shift(GROUP * group + g)) % NZ for g in range(GROUP)]
+        rows = BLK * SUB
+
+        def stacked(ref):
+            return jnp.concatenate([ref(src).reshape(rows, -1) for src in srcs], axis=0)
+
+        rhs = (a2 if level else a1)[...].reshape(KW, 256)
+        prod = jnp.dot(stacked(lambda src: w[level, :, src]), rhs, preferred_element_type=F32)
+        for g, src in enumerate(srcs):
+            anchor = a1[pl.ds(base, BLK), src].reshape(rows, 256).astype(F32)
+            before = cur1[:, src].reshape(rows, 256).astype(F32) if level else anchor
+            nxt = (anchor * prod[g * rows : (g + 1) * rows] + before).astype(BF16).reshape(BLK, SUB, 256)
+            if level:
+                cur2[:, src] = nxt
+            else:
+                cur1[:, src] = nxt
+
+        for g, src in enumerate(srcs):
+            if level:
+                crossed(src)
+            else:
+                second_send(GROUP * group + g)
 
     def rows_here(level, s):
         src = (z + NZ - slot_shift(s)) % NZ
@@ -400,9 +399,23 @@
         def _():
             arrived(w.at[level, :, src, :, pl.ds(0, 3 * KA)], dy_r.at[level, s])
 
-        @pl.when(c == tall)
-        def _():
-            arrived(w.at[level, :, src, :, rest], db_r.at[level, s])
+    def each(low, high, step):
+        @pl.loop(low, high)
+        def _(s):
+            step(s)
+
+    def at(i, plan, step):
+        for due, low, high in plan:
+            @pl.when(i == due)
+            def _():
+                each(low, high, step)
+
+    def layers(level, low, high):
+        @pl.loop(low // GROUP, high // GROUP)
+        def _(k):
+            for g in range(GROUP):
+                rows_here(level, GROUP * k + g)
+            layer(level, k)
 
     @pl.when(c == wide)
     def _():
@@ -415,7 +428,7 @@
         hand_over(1, 0)
         examples_out(1, 3)
 
-        @pl.loop(1, 14)
+        @pl.loop(1, 13)
         def _(i):
             @pl.when(i < NZ)
             def _():
@@ -426,37 +439,31 @@
                 def _():
                     examples_out(low, high)
 
-            @pl.when((i >= 4) & (i < 12))
-            def _():
-                from_b(0, i - 4)
+            @pl.when((i >= 2) & (i < 10))
+            def _():
+                from_b(0, i - 2)
 
             @pl.when(i >= 6)
             def _():
                 from_a(1, i - 6)
 
-            @pl.when((i >= 5) & (i < 13))
-            def _():
-                relay_step(i - 5)
-
-            @pl.when(i == 10)
+            at(i, ((5, 0, 1), (6, 1, 2), (7, 2, 3), (8, 3, 4), (9, 4, 6), (10, 6, 8)), relay_step)
+
+            @pl.when(i == 8)
             def _():
                 tower_step(0)
 
-            @pl.when(i >= 11)
-            def _():
-                from_b(1, i - 11)
-
-        tower_step(1)
-        tower_step(2)
-
-        @pl.loop(0, NZ)
-        def _(i):
-            far_step(i)
-
-        @pl.loop(0, NZ)
-        def _(s):
-            rows_here(0, s)
-            layer(0, s)
+            @pl.when(i == 11)
+            def _():
+                from_b(1, 0)
+                tower_step(1)
+                tower_step(2)
+                each(0, NZ, far_step)
+                layers(0, 0, 4)
+
+        layers(0, 4, NZ)
+        each(1, 3, functools.partial(from_b, 1))
+        from_a(1, 7)
 
     @pl.when(c == tall)
     def _():
@@ -471,7 +478,7 @@
         example_step(0)
         from_y(0, 0)
 
-        @pl.loop(1, 12)
+        @pl.loop(1, 11)
         def _(i):
             @pl.when(i < NZ)
             def _():
@@ -490,116 +497,100 @@
             def _():
                 from_y(0, i - 1)
 
-            @pl.when((i > 1) & (i < NZ + 1))
-            def _():
-                example_step(i - 1)
+            at(i, ((2, 1, 2), (3, 2, 3), (4, 3, 5), (5, 5, 7), (6, 7, 8)), example_step)
 
             @pl.when(i >= 8)
             def _():
                 to_y(1, i - 7)
 
-            @pl.when(i >= 10)
-            def _():
-                from_y(1, i - 9)
-
-            @pl.when(i == 11)
-            def _():
-                @pl.loop(5, NZ)
-                def _(s):
-                    to_y(1, s)
-
-            @pl.when((i >= 3) & (i < 11))
+            @pl.when(i >= 3)
             def _():
                 to_core(0, i - 3)
 
-            @pl.when((i >= 3) & (i < 11))
-            def _():
-                relay_step(i - 3)
+            at(i, ((3, 0, 1), (4, 1, 2), (5, 2, 3), (6, 3, 5), (7, 5, 7), (8, 7, 8)), relay_step)
 
             @pl.when(i == 4)
             def _():
                 to_core(1, 0)
 
-            @pl.when(i == 8)
+            @pl.when(i == 5)
             def _():
                 tower_step(0)
 
-            @pl.when(i == 11)
+            @pl.when(i == 9)
             def _():
                 tower_step(1)
                 tower_step(2)
-
-            @pl.when(i >= 10)
-            def _():
-                @pl.loop(0, 3)
-                def _(k):
-                    s = 3 * (i - 10) + k
-                    rows_here(0, s)
-                    layer(0, s)
-
-        @pl.loop(6, NZ)
-        def _(s):
-            rows_here(0, s)
-            layer(0, s)
+                arrived(w.at[0, :, :, :, rest], db_r.at[0])
+                layers(0, 0, 4)
+
+        to_y(1, 4)
+        layers(0, 4, NZ)
 
     @pl.when(c == wide)
     def _():
-        @pl.loop(0, NZ)
+        each(0, 3, second_step)
+        each(3, 5, functools.partial(from_b, 1))
+        each(3, 5, tower_step)
+        each(3, NZ, second_step)
+        each(5, 7, functools.partial(from_b, 1))
+        each(5, 7, tower_step)
+        from_b(1, 7)
+
+    @pl.when(c == tall)
+    def _():
+        @pl.loop(1, NZ)
         def _(i):
-            @pl.when((i % 4 == 0) | (i % 4 == 1))
-            def _():
-                k = 3 + 2 * (i // 4) + i % 4
-                from_b(1, k)
-                tower_step(k)
-
-            second_step(i)
-
-        from_b(1, 7)
-        tower_step(7)
-
-    @pl.when(c == tall)
-    def _():
-        @pl.loop(5, 10)
-        def _(i):
-            from_y(1, i - 2)
-            to_core(1, i - 4)
-
-            @pl.when(i < 9)
-            def _():
-                second_step(2 * i - 10)
-                second_step(2 * i - 9)
-
-            @pl.when(i >= 6)
-            def _():
-                tower_step(i - 3)
-
-        to_core(1, 6)
-        tower_step(7)
+            from_y(1, i)
+
+            @pl.when(i < 4)
+            def _():
+                to_y(1, i + 4)
+
+            for due, low, high in ((2, 3, 5), (5, 5, 7), (7, 7, 8)):
+                @pl.when(i == due)
+                def _():
+                    each(low, high, tower_step)
+
+            @pl.when((i > 1) & (i < 6))
+            def _():
+                each(2 * i - 4, 2 * i - 2, second_step)
+
+            @pl.when(i >= 4)
+            def _():
+                to_core(1, i - 3)
+
+        to_core(1, 5)
+        arrived(w.at[1, :, :, :, rest], db_r.at[1])
 
     @pl.loop(0, NZ)
     def _(s):
         second_far(s)
 
-    @pl.loop(0, NZ)
-    def _(s):
-        @pl.when((c == tall) & (s == 4))
-        def _():
-            to_core(1, 7)
-            got = cands.at[pl.ds(NX * y, NX)]
-            arrived(cands.at[pl.ds(NX * y, NX - 1)], c_r.at[0])
-            for step in range(1, NX):
-                copy(got, got, c_s.at[1], c_r.at[1], {"batch_0": (y + step) % NX}).start()
-
-        rows_here(1, s)
-        layer(1, s)
+    layers(1, 0, 4)
+
+    @pl.when(c == wide)
+    def _():
+        tower_step(7)
+
+    @pl.when(c == tall)
+    def _():
+        to_core(1, 6)
+        to_core(1, 7)
+        got = cands.at[pl.ds(NX * y, NX)]
+        arrived(cands.at[pl.ds(NX * y, NX - 1)], c_r.at[0])
+        for step in range(1, NX):
+            copy(got, got, c_s.at[1], c_r.at[1], {"batch_0": (y + step) % NX}).start()
+
+    layers(1, 4, NZ)
 
     arrived(t.at[:, c], td_r)
 
     def tower(k):
-        lhs = t[k, :, :, 0 : BLK * 128].reshape(128, BLK * 128)
+        lhs = t[pl.ds(2 * k, 2), :, :, 0 : BLK * 128].reshape(256, BLK * 128)
         prod = jnp.dot(lhs, cur2[...].reshape(BLK * 128, 256), preferred_element_type=F32)
-        part[pl.ds(128 * k, 128)] = prod.astype(BF16)
-        mine[pl.ds(128 * k, 128)] = prod
+        part[pl.ds(256 * k, 256)] = prod.astype(BF16)
+        mine[pl.ds(256 * k, 256)] = prod
 
     def far_sum(h):
         for j in range(2):
@@ -611,7 +602,7 @@
                 ).start()
 
     for h in range(2):
-        @pl.loop(4 * h, 4 * h + 4)
+        @pl.loop(2 * h, 2 * h + 2)
         def _(k):
             tower(k)
 
@@ -672,7 +663,7 @@
         wanted = target[pl.ds(z, 1), :]
         index = lax.broadcasted_iota(jnp.int32, (256, 128), 0)
 
-        def sums(k, carry):
+        def fold(k, carry):
             total, picked = carry
             got = logits[k]
             e = jnp.exp(got - top)
@@ -683,7 +674,7 @@
             )
 
         zero = jnp.zeros((8, 128), F32)
-        total, picked = lax.fori_loop(0, NX * NX, sums, (zero, zero), unroll=4)
+        total, picked = lax.fori_loop(0, NX * NX, fold, (zero, zero), unroll=4)
         total = jnp.sum(total, axis=0, keepdims=True)
         picked = jnp.sum(picked, axis=0, keepdims=True)
         result = top + jnp.log(total) - picked
@@ -736,16 +727,13 @@
             arrived(a1.at[pl.ds(0, HALF), :, :, pl.ds(0, 128)], ag1_ls.at[1])
 
     for d in range(2):
-        arrived(a2.at[pl.ds(0, 6)], ag2_s.at[0, d])
-        arrived(a2.at[0, pl.ds(0, 4)], ag2_s.at[1, d])
-        arrived(a2.at[pl.ds(0, 6), pl.ds(0, 4)], ag2_ls.at[0, d])
-        arrived(a2.at[0, pl.ds(0, 2)], ag2_ls.at[1, d])
+        arrived(a2.at[pl.ds(0, HALF), pl.ds(0, 4)], ag2_s.at[d])
+        arrived(a2.at[pl.ds(0, HALF), pl.ds(0, 2)], ag2_ls.at[d])
     for d in range(2):
         arrived(t.at[pl.ds(0, 3), 0], t_s.at[d])
         arrived(t.at[0, 0, pl.ds(0, 32)], t_s.at[2 + d])
     arrived(t.at[:, 0], td_s)
-    arrived(cur2.at[pl.ds(0, 6)], o_s.at[0])
-    arrived(cur2.at[0, pl.ds(0, 4)], o_s.at[1])
+    arrived(a1.at[pl.ds(0, HALF), :, :, pl.ds(0, 128)], o_s)
     for k in range(NZ):
         loss_out[k : k + 1] = loss[k, 0:1]
     arrived(out, o_r)
@@ -779,18 +767,18 @@
             pltpu.VMEM((NX * NX, 256, 128), F32),
             pltpu.VMEM((128, 128), BF16),
             pltpu.VMEM((NZ, 8, 128), F32),
-            dma((2, NY + NREST - 1)), dma((BLK,)), dma,
+            dma((2,)), dma, dma,
             dma((2,)), dma((NZ,)),
-            dma((2,)), dma((2, NZ, 2)), dma((2,)),
-            dma((2, 2)), dma((2, NZ, 2)), dma((2, 2)), dma((2, NZ)),
+            dma((2,)), dma((2, NZ)), dma((2,)),
+            dma((2,)), dma((NZ, 2)), dma((2,)), dma((NZ,)),
             dma((2, 2, 2)), dma((2, NZ, 2)),
             dma((2, 2)), dma((2, NZ, 2)),
-            dma((2, 2)), dma((2, NZ, 2)),
-            dma((2,)), dma((2, NZ)), dma((2,)), dma((2, NZ)), dma((2,)), dma((2, NZ)),
+            dma((2, 2)), dma((2, NZ)),
+            dma((2,)), dma((2, NZ)), dma((2,)), dma((2,)), dma((2,)), dma((2, NZ)),
             dma((4,)), dma((9,)), dma, dma,
             dma((2,)), dma((2,)),
             dma((4,)), dma, dma,
-            dma((2,)), dma,
+            dma, dma,
             dma((3,)), dma,
         ],
         compiler_params=pltpu.CompilerParams(collective_id=0, has_side_effects=True, vmem_limit_bytes=60 * 1024 * 1024),

time: 95.5 us -> 92.1 us (0.964)
  Pallas kernels: 92.6 us -> 89.1 us
    pallas_call x1, Pallas kernels: 92.6 us -> 89.1 us  [body(): pl.pallas_call(kernel, out_shape=(pltpu.VMEM((HALF, SUB, 1024), BF16), pl...]
where the time goes in v4:
time: 92.1 us; the launch traced here: 91.1 us
  Pallas kernels  89.1 us (97%)
  local copies, waits for them, and re-layouts  1.35 us (1%)
    pallas_call x1, Pallas kernels, body(): pl.pallas_call(kernel, out_shape=(pltpu.VMEM((HALF, SUB, 1024), BF16), pl...  89.1 us

profile of v4, /device:TPU:7, one launch (start us, length us, event | category | flops | bytes accessed | tf_op | source)
XLA Modules:
  0.0 91.1 jit_solution(5481199877123604919)
XLA Ops:
  0.6 89.1 %dcn.1 = (bf16[13,16,1024]{2,1,0:T(8,128)(2,1)S(1)}, f32[8,128]{1,0:T(8,128)S(1)}) custom-call(bf16[13,16,1024]{2,1,0:T(8,128)(2,1)} %feat.1, bf16[2,13,26,16,128]{4,3,2,1,0:T(8,128)(2,1)} %bitcast.7, f32[13,2,16]{2,1,0:T(2,128)} %bitcast.9, bf16[26,64,128]{2,1,0:T(8,128)(2,1)} %bitcast.8, f32[1,64]{1,0:T(1,128)} %bitcast.11, bf16[64,128]{1,0:T(8,128)(2,1)} %q_w.1, ...), custom_call_target="tpu_custom_call" | custom-call | tf_op jit(solution)/shard_map/dcn/pallas_call | solution.py:746
  89.7 0.8 copy.13
  90.5 0.6 copy.14

commit v5 on v4

--- a/solution.py
+++ b/solution.py
@@ -357,16 +357,25 @@
 
         owned((x + 2) % NX, src, act)
 
-    def crossed(to):
+    def crossed(to, j):
         def act(field, n):
-            for j in range(2):
-                copy(
-                    cur2.at[pl.ds(field - base, n), to, :, lanes(j)],
-                    out.at[pl.ds(field - HALF * wide, n), :, lanes(z)],
-                    o_s, o_r, {"batch_1": first + j, "dim": to, "field": wide},
-                ).start()
+            copy(
+                cur2.at[pl.ds(field - base, n), to, :, lanes(j)],
+                out.at[pl.ds(field - HALF * wide, n), :, lanes(z)],
+                o_s, o_r, {"batch_1": first + j, "dim": to, "field": wide},
+            ).start()
 
         owned(x, to, act)
+
+    def crossed_away(to):
+        @pl.when(c == wide)
+        def _():
+            crossed(to, 0)
+            crossed(to, 1)
+
+        @pl.when(c == tall)
+        def _():
+            crossed(to, 1 - p)
 
     def layer(level, group):
         srcs = [(z + NZ - slot_shift(GROUP * group + g)) % NZ for g in range(GROUP)]
@@ -388,7 +397,13 @@
 
         for g, src in enumerate(srcs):
             if level:
-                crossed(src)
+                @pl.when(c == tall)
+                def _():
+                    crossed(src, p)
+
+                @pl.when(GROUP * group < 4)
+                def _():
+                    crossed_away(src)
             else:
                 second_send(GROUP * group + g)
 
@@ -447,22 +462,29 @@
             def _():
                 from_a(1, i - 6)
 
-            at(i, ((5, 0, 1), (6, 1, 2), (7, 2, 3), (8, 3, 4), (9, 4, 6), (10, 6, 8)), relay_step)
+            at(i, ((5, 0, 1), (6, 1, 2), (7, 2, 4), (8, 4, 7), (9, 7, 8)), relay_step)
 
             @pl.when(i == 8)
             def _():
                 tower_step(0)
 
+            @pl.when(i == 7)
+            def _():
+                from_b(1, 0)
+
             @pl.when(i == 11)
             def _():
-                from_b(1, 0)
                 tower_step(1)
                 tower_step(2)
+
+            @pl.when(i == 10)
+            def _():
+                each(1, 3, functools.partial(from_b, 1))
                 each(0, NZ, far_step)
                 layers(0, 0, 4)
 
         layers(0, 4, NZ)
-        each(1, 3, functools.partial(from_b, 1))
+        each(3, 5, functools.partial(from_b, 1))
         from_a(1, 7)
 
     @pl.when(c == tall)
@@ -529,10 +551,9 @@
 
     @pl.when(c == wide)
     def _():
-        each(0, 3, second_step)
-        each(3, 5, functools.partial(from_b, 1))
+        each(0, 2, second_step)
         each(3, 5, tower_step)
-        each(3, NZ, second_step)
+        each(2, NZ, second_step)
         each(5, 7, functools.partial(from_b, 1))
         each(5, 7, tower_step)
         from_b(1, 7)
@@ -592,21 +613,19 @@
         part[pl.ds(256 * k, 256)] = prod.astype(BF16)
         mine[pl.ds(256 * k, 256)] = prod
 
-    def far_sum(h):
+    def far_sum(k):
         for j in range(2):
             @pl.when((x + NX - first - j) % NX == 2)
             def _():
-                to = (xr, xl)[h]
                 copy(
-                    part.at[pl.ds(512 * h, 512), pl.ds(128 * j, 128)], hop, rs_s.at[h], hop_r, {"batch_1": to}
+                    part.at[pl.ds(256 * k, 256), pl.ds(128 * j, 128)],
+                    hop.at[pl.ds(256 * (k % 2), 256)],
+                    rs_s.at[k // 2], hop_r.at[k % 2], {"batch_1": (xr, xl)[k // 2]},
                 ).start()
 
-    for h in range(2):
-        @pl.loop(2 * h, 2 * h + 2)
-        def _(k):
-            tower(k)
-
-        far_sum(h)
+    for k in range(4):
+        tower(k)
+        far_sum(k)
 
     for r, own, added, way in ((1, 0, 512, xl), (3, 512, 0, xr)):
         for j in range(2):
@@ -617,9 +636,13 @@
                 copy(
                     part.at[pl.ds(own, 512), cols], slot.at[pl.ds(own, 512)], rs_s.at[2], rs_r, {"batch_1": way}
                 ).start()
-                arrived(hop, hop_r)
-                summed[...] = (mine[pl.ds(added, 512), cols] + hop[...].astype(F32)).astype(BF16)
-                copy(summed, slot.at[pl.ds(added, 512)], rs_s.at[3], rs_r, {"batch_1": way}).start()
+                for q in range(2):
+                    here, there = pl.ds(256 * q, 256), pl.ds(added + 256 * q, 256)
+                    arrived(hop.at[here], hop_r.at[q])
+                    summed[here] = (mine[there, cols] + hop[here].astype(F32)).astype(BF16)
+                    copy(summed.at[here], slot.at[there], rs_s.at[3], rs_r, {"batch_1": way}).start()
+
+    each(4, NZ, lambda s: crossed_away((z + NZ - slot_shift(s)) % NZ))
 
     @pl.when(c == tall)
     def _():
@@ -777,7 +800,7 @@
             dma((2,)), dma((2, NZ)), dma((2,)), dma((2,)), dma((2,)), dma((2, NZ)),
             dma((4,)), dma((9,)), dma, dma,
             dma((2,)), dma((2,)),
-            dma((4,)), dma, dma,
+            dma((4,)), dma, dma((2,)),
             dma, dma,
             dma((3,)), dma,
         ],

time: 92.1 us -> 88.7 us (0.963)
  Pallas kernels: 89.1 us -> 86.6 us
    pallas_call x1, Pallas kernels: 89.1 us -> 86.6 us  [body(): pl.pallas_call(kernel, out_shape=(pltpu.VMEM((HALF, SUB, 1024), BF16), pl...]
where the time goes in v5:
time: 88.7 us; the launch traced here: 88.6 us
  Pallas kernels  86.6 us (98%)
  local copies, waits for them, and re-layouts  1.35 us (2%)
    pallas_call x1, Pallas kernels, body(): pl.pallas_call(kernel, out_shape=(pltpu.VMEM((HALF, SUB, 1024), BF16), pl...  86.6 us

profile of v5, /device:TPU:7, one launch (start us, length us, event | category | flops | bytes accessed | tf_op | source)
XLA Modules:
  0.0 88.6 jit_solution(14649340966049065564)
XLA Ops:
  0.6 86.6 %dcn.1 = (bf16[13,16,1024]{2,1,0:T(8,128)(2,1)S(1)}, f32[8,128]{1,0:T(8,128)S(1)}) custom-call(bf16[13,16,1024]{2,1,0:T(8,128)(2,1)} %feat.1, bf16[2,13,26,16,128]{4,3,2,1,0:T(8,128)(2,1)} %bitcast.7, f32[13,2,16]{2,1,0:T(2,128)} %bitcast.9, bf16[26,64,128]{2,1,0:T(8,128)(2,1)} %bitcast.8, f32[1,64]{1,0:T(1,128)} %bitcast.11, bf16[64,128]{1,0:T(8,128)(2,1)} %q_w.1, ...), custom_call_target="tpu_custom_call" | custom-call | tf_op jit(solution)/shard_map/dcn/pallas_call | solution.py:769
  87.2 0.8 copy.13
  88.0 0.6 copy.14

commit v6 on v5

--- a/solution.py
+++ b/solution.py
@@ -551,9 +551,9 @@
 
     @pl.when(c == wide)
     def _():
-        each(0, 2, second_step)
+        each(0, 4, second_step)
         each(3, 5, tower_step)
-        each(2, NZ, second_step)
+        each(4, NZ, second_step)
         each(5, 7, functools.partial(from_b, 1))
         each(5, 7, tower_step)
         from_b(1, 7)
@@ -573,9 +573,9 @@
                 def _():
                     each(low, high, tower_step)
 
-            @pl.when((i > 1) & (i < 6))
-            def _():
-                each(2 * i - 4, 2 * i - 2, second_step)
+            @pl.when(i < 5)
+            def _():
+                each(2 * i - 2, 2 * i, second_step)
 
             @pl.when(i >= 4)
             def _():

time: 88.7 us -> 87.8 us (0.990)
  Pallas kernels: 86.6 us -> 85.7 us
    pallas_call x1, Pallas kernels: 86.6 us -> 85.7 us  [body(): pl.pallas_call(kernel, out_shape=(pltpu.VMEM((HALF, SUB, 1024), BF16), pl...]
where the time goes in v6:
time: 87.8 us; the launch traced here: 87.7 us
  Pallas kernels  85.7 us (98%)
  local copies, waits for them, and re-layouts  1.35 us (2%)
    pallas_call x1, Pallas kernels, body(): pl.pallas_call(kernel, out_shape=(pltpu.VMEM((HALF, SUB, 1024), BF16), pl...  85.7 us

profile of v6, /device:TPU:7, one launch (start us, length us, event | category | flops | bytes accessed | tf_op | source)
XLA Modules:
  0.0 87.7 jit_solution(15639381222380374605)
XLA Ops:
  0.6 85.7 %dcn.1 = (bf16[13,16,1024]{2,1,0:T(8,128)(2,1)S(1)}, f32[8,128]{1,0:T(8,128)S(1)}) custom-call(bf16[13,16,1024]{2,1,0:T(8,128)(2,1)} %feat.1, bf16[2,13,26,16,128]{4,3,2,1,0:T(8,128)(2,1)} %bitcast.7, f32[13,2,16]{2,1,0:T(2,128)} %bitcast.9, bf16[26,64,128]{2,1,0:T(8,128)(2,1)} %bitcast.8, f32[1,64]{1,0:T(1,128)} %bitcast.11, bf16[64,128]{1,0:T(8,128)(2,1)} %q_w.1, ...), custom_call_target="tpu_custom_call" | custom-call | tf_op jit(solution)/shard_map/dcn/pallas_call | solution.py:769
  86.3 0.8 copy.13
  87.1 0.6 copy.14
